TPU v7x, 32 devices: a whole 2x2x4 slice. The times are simulated.
32 devices in a mesh: fy: 4 (over y, core), fx: 4 (over z), blk: 2 (over x).
Axes of the slice: x: 2, y: 2, z: 4, core: 2. Of those that a mesh axis runs over, the one named last changes fastest.
Arguments:
- sky_image: bfloat16 [8, 512, 512], P('blk', 'fy', 'fx'), may hold values from -33 to 33
- vis_data: bfloat16 [4, 4, 8, 2, 512], P('fy', 'fx', 'blk'), may hold values from -6 to 6
- interp_weights: bfloat16 [4, 4, 2, 4, 2, 128, 128], P('fy', 'fx'), may hold values from -0.25 to 0.25
- tile_rows: int32 [4, 4, 2, 4, 2], P('fy', 'fx'), may hold values from 0 to 127
- facet_list: int32 [4, 4, 2], P('fy', 'fx'), may hold values from 0 to 3, as said below
- vis_count: int32 [4, 4], P('fy', 'fx'), may hold values from 128 to 512
- wavelet_threshold: float32 [4, 8], P(None, 'blk'), may hold values from 0.05 to 0.5
- spectral_weight: float32 [], replicated, may hold values from 0.1 to 1
Outputs:
- restored: float32 [8, 512, 512], P('blk', 'fy', 'fx')
Inputs may be any that keep to these rules, and one draw needn't show every extreme that they name: `facet_list`: the 2 facet numbers of one block are distinct.
All inputs are finite; a program needn't handle non-finite values.
Results may differ from a plain program's by a relative error of at most 0.0035.
Values may be sent and summed in bfloat16 or wider, within the bound.
A program may use at most 64 MiB of HBM per device.

v0:
```python
import math

import jax
import jax.numpy as jnp
from jax import lax
from jax.sharding import PartitionSpec as P

top_precision = lax.Precision.HIGHEST
descent_step = 2.0


def extended(cells, sides, width):
    for axis, dim in sides:
        count = lax.axis_size(axis)
        ends = count - 1
        head = lax.slice_in_dim(cells, 0, width, axis=dim)
        tail = lax.slice_in_dim(cells, cells.shape[dim] - width, cells.shape[dim], axis=dim)
        cells = jnp.concatenate(
            [
                lax.ppermute(tail, axis, [(i, (i + 1) % count) for i in range(ends)]),
                cells,
                lax.ppermute(head, axis, [((i + 1) % count, i) for i in range(ends)]),
            ],
            axis=dim,
        )
    return cells


def dft_tables(length):
    positions = jnp.arange(length, dtype=jnp.int32)
    phases = positions[:, None] * positions[None, :] % length
    angles = phases.astype(jnp.float32) * (2.0 * math.pi / length)
    scaling = 1.0 / math.sqrt(length)
    cosine = jnp.cos(angles) * scaling
    sinus_table = jnp.sin(angles) * scaling
    left_table = jnp.concatenate([cosine, -sinus_table], axis=0)
    right_table = jnp.stack(
        [
            jnp.concatenate([cosine, -sinus_table], axis=1),
            jnp.concatenate([sinus_table, cosine], axis=1),
        ]
    )
    return (left_table, right_table)


def forward_transform(facets, left_table, right_table):
    halfway = jnp.einsum(
        "wy,fcyx->fcwx", left_table.astype(jnp.bfloat16), facets, preferred_element_type=jnp.float32
    ).astype(jnp.bfloat16)
    facet_count, channel_count, doubled, facet_width = halfway.shape
    halfway = halfway.reshape(facet_count, channel_count, 2, doubled // 2, facet_width)
    spectra = jnp.einsum(
        "fcpux,pxw->fcuw",
        halfway,
        right_table.astype(jnp.bfloat16),
        preferred_element_type=jnp.float32,
    )
    return spectra.astype(jnp.bfloat16)


def adjoint_transform(spectrum_grad, left_table, right_table):
    halfway = jnp.einsum("fcuw,pxw->fcpux", spectrum_grad, right_table, precision=top_precision)
    facet_count, channel_count, parts_two, facet_width, other_width = halfway.shape
    halfway = halfway.reshape(facet_count, channel_count, 2 * facet_width, other_width)
    return jnp.einsum("wy,fcwx->fcyx", left_table, halfway, precision=top_precision)


def pick_rows(spectrum_one, row_ids):
    return jnp.take(spectrum_one, row_ids, axis=1)


def block_rows(chosen, block_vis, block_weights, block_tiles, block_count):
    picked = jax.vmap(pick_rows)(chosen, block_tiles)
    facet_count, channel_count, tile_count, slot_count, doubled = picked.shape
    picked = picked.reshape(facet_count, channel_count, tile_count, slot_count, 2, doubled // 2)
    predicted = jnp.einsum(
        "fanjv,fcanpv->cpaj", block_weights, picked, preferred_element_type=jnp.float32
    )
    predicted = predicted.reshape(channel_count, 2, -1)
    live_mask = jnp.arange(predicted.shape[2], dtype=jnp.int32) < block_count
    residual = jnp.where(live_mask, predicted - block_vis.astype(jnp.float32), 0.0).astype(
        jnp.bfloat16
    )
    residual = residual.reshape(channel_count, 2, tile_count, -1)
    contrib = jnp.einsum(
        "fanjv,cpaj->fancpv", block_weights, residual, preferred_element_type=jnp.float32
    )
    return contrib.reshape(facet_count, tile_count, slot_count, channel_count, doubled)


def smooth_axis(values, stride, axis_id):
    widths = [(0, 0), (0, 0), (0, 0)]
    widths[axis_id] = (stride, stride)
    padded = jnp.pad(values, widths)
    length = values.shape[axis_id]
    below_rows = lax.slice_in_dim(padded, 0, length, axis=axis_id)
    above_rows = lax.slice_in_dim(padded, 2 * stride, 2 * stride + length, axis=axis_id)
    return (below_rows + 2.0 * values + above_rows) * 0.25


def smooth_both(values, stride):
    return smooth_axis(smooth_axis(values, stride, 1), stride, 2)


def shrink_matrix(gram_matrix, offset):
    dimension = gram_matrix.shape[0]
    shifted = gram_matrix + offset * jnp.eye(dimension, dtype=jnp.float32)
    positions = jnp.arange(dimension, dtype=jnp.int32)
    columns = []
    for column_id in range(dimension):
        if column_id > 0:
            earlier = jnp.stack(columns, axis=1)
            correction = jnp.sum(earlier * earlier[column_id][None, :], axis=1)
        else:
            correction = jnp.zeros((dimension,), jnp.float32)
        pivot = jnp.sqrt(shifted[column_id, column_id] - correction[column_id])
        column = (shifted[:, column_id] - correction) / pivot
        columns.append(jnp.where(positions >= column_id, column, 0.0))
    factor = jnp.stack(columns, axis=1)
    forward_rows = []
    for row_id in range(dimension):
        accum = gram_matrix[row_id]
        if row_id > 0:
            accum = accum - jnp.sum(
                factor[row_id, :row_id][:, None] * jnp.stack(forward_rows, axis=0), axis=0
            )
        forward_rows.append(accum / factor[row_id, row_id])
    backward_rows = [None] * dimension
    for row_id in range(dimension - 1, -1, -1):
        accum = forward_rows[row_id]
        if row_id < dimension - 1:
            later = jnp.stack(backward_rows[row_id + 1 :], axis=0)
            accum = accum - jnp.sum(factor[row_id + 1 :, row_id][:, None] * later, axis=0)
        backward_rows[row_id] = accum / factor[row_id, row_id]
    return jnp.stack(backward_rows, axis=0)


def body(
    sky_image,
    vis_data,
    interp_weights,
    tile_rows,
    facet_list,
    vis_count,
    wavelet_threshold,
    spectral_weight,
):
    channel_count, facet_width, other_width = sky_image.shape
    left_table, right_table = dft_tables(facet_width)
    chosen_ids = facet_list[0, 0]
    block_tiles = tile_rows[0, 0]
    row_images = lax.all_gather(sky_image[None], "fx", axis=0, tiled=True)
    chosen = forward_transform(jnp.take(row_images, chosen_ids, axis=0), left_table, right_table)
    contrib = block_rows(chosen, vis_data[0, 0], interp_weights[0, 0], block_tiles, vis_count[0, 0])
    facet_count, tile_count, slot_count, chan_here, doubled = contrib.shape
    row_total = lax.axis_size("fx")
    selector = (chosen_ids[:, None] == jnp.arange(row_total, dtype=jnp.int32)[None, :]).astype(
        jnp.float32
    )
    flat_rows = contrib.reshape(facet_count, tile_count * slot_count, chan_here, doubled)
    outgoing = jnp.einsum("fk,frcw->krcw", selector, flat_rows, precision=top_precision)
    row_lists, facet_lists = (
        lax.all_gather(block_tiles[None], "fx", axis=0, tiled=True),
        lax.all_gather(chosen_ids[None], "fx", axis=0, tiled=True),
    )
    matched = (facet_lists == lax.axis_index("fx")).astype(jnp.int32)
    source_rows = jnp.sum(matched[:, :, None, None] * row_lists, axis=1).reshape(
        row_total, tile_count * slot_count
    )
    incoming = lax.all_to_all(
        outgoing.astype(jnp.bfloat16), "fx", split_axis=0, concat_axis=0, tiled=True
    ).astype(outgoing.dtype)
    placement = (source_rows[..., None] == jnp.arange(doubled // 2, dtype=jnp.int32)).astype(
        jnp.float32
    )
    own_grad = jnp.einsum("jru,jrcw->cuw", placement, incoming, precision=top_precision)
    gradient = adjoint_transform(own_grad[None], left_table, right_table)[0]
    stepped = sky_image.astype(jnp.float32) - descent_step * gradient
    levels = wavelet_threshold.shape[0]
    coarse = stepped
    clipped_sum = jnp.zeros_like(stepped)
    for level_index in range(levels):
        stride = 2**level_index
        padded = extended(coarse.astype(jnp.bfloat16), (("fy", 1), ("fx", 2)), stride).astype(
            coarse.dtype
        )
        smoother = smooth_both(padded, stride)[
            :, stride : stride + facet_width, stride : stride + other_width
        ]
        bound_now = wavelet_threshold[level_index][:, None, None]
        clipped_sum = clipped_sum + jnp.clip(coarse - smoother, -bound_now, bound_now)
        coarse = smoother
    shrunk = stepped - clipped_sum
    offset = spectral_weight * (facet_width * other_width)
    all_channels = lax.all_gather(shrunk, "blk", axis=0, tiled=True)
    gram_matrix = jnp.einsum("cyx,dyx->cd", all_channels, all_channels, precision=top_precision)
    matrix = shrink_matrix(gram_matrix, offset)
    own_cols = lax.dynamic_slice_in_dim(
        matrix, lax.axis_index("blk") * channel_count, channel_count, 1
    )
    result = jnp.einsum("cyx,cd->dyx", all_channels, own_cols, precision=top_precision)
    return result


def solution(mesh):
    in_specs = (
        P("blk", "fy", "fx"),
        P("fy", "fx", "blk", None, None),
        P("fy", "fx", None, None, None, None, None),
        P("fy", "fx", None, None, None),
        P("fy", "fx", None),
        P("fy", "fx"),
        P(None, "blk"),
        P(),
    )
    out_specs = P("blk", "fy", "fx")
    return jax.shard_map(body, mesh=mesh, in_specs=in_specs, out_specs=out_specs, check_vma=False)
```

profile of v0, /device:TPU:28, one launch (start us, length us, event | category | flops | bytes accessed | tf_op | source)
XLA Modules:
  0.0 175.9 jit_solution(17622049769280057704)
XLA Ops:
  0.0 0.7 fusion.69
  1.7 16.4 %all-gather = bf16[16,128,128]{2,1,0:T(8,128)(2,1)S(1)} all-gather(bf16[4,128,128]{2,1,0:T(8,128)(2,1)S(1)} %copy-done.6), channel_id=2, replica_groups=mesh['fy'=4,'fx'=4,'blk'=2] {'fx'}, dimensions={0}, use_global_device_ids=true | all-gather | bytes 655360 | tf_op jit(solution)/shard_map/all_gather | solution.py:152
  20.4 0.6 gather_fusion.1
  23.4 0.7 copy.154
  24.1 5.1 %all-to-all-start = ((bf16[4,8,4,256]{3,2,1,0:T(4,128)(2,1)}), bf16[4,8,4,256]{3,2,1,0:T(4,128)(2,1)S(1)}, u32[]{:S(2)}, u32[]{:S(2)}) async-start(bf16[4,8,4,256]{3,2,1,0:T(4,128)(2,1)} %copy.154), calls=%async_computation | async-start | bytes 131072 | tf_op jit(solution)/shard_map/all_to_all | solution.py:170
  29.2 10.6 %all-gather.2 = s32[4,1,2,4,2]{3,4,2,1,0:T(2,128)S(1)} all-gather(s32[1,1,2,4,2]{3,4,2,1,0:T(2,128)S(1)} %copy-done.7), channel_id=4, replica_groups=mesh['fy'=4,'fx'=4,'blk'=2] {'fx'}, dimensions={0}, use_global_device_ids=true | all-gather | bytes 320 | tf_op jit(solution)/shard_map/all_gather | solution.py:163
  39.8 7.6 %all-gather.1 = s32[4,1,2]{2,1,0:T(1,128)S(1)} all-gather(s32[1,1,2]{2,1,0:T(1,128)S(1)} %copy-done.10), channel_id=3, replica_groups=mesh['fy'=4,'fx'=4,'blk'=2] {'fx'}, dimensions={0}, use_global_device_ids=true | all-gather | bytes 40 | tf_op jit(solution)/shard_map/all_gather | solution.py:164
  48.0 1.0 convolution_bitcast_fusion.2
  49.1 1.2 fusion.112
  50.3 1.9 %collective-permute-start.1 = (bf16[4,1,128]{2,1,0:T(2,128)(2,1)S(1)}, bf16[4,1,128]{2,1,0:T(2,128)(2,1)S(1)}, u32[]{:S(2)}, u32[]{:S(2)}) collective-permute-start(bf16[4,1,128]{2,1,0:T(2,128)(2,1)S(1)} %get-tuple-element.47), channel_id=1, source_target_pairs={{8,0},{16,8},{24,16},{9,1},{17,9},{25,17},{10,2},{18,10},{26,18},{... | collective-permute-start | bytes 3080 | tf_op jit(solution)/shard_map/ppermute | solution.py:22
  52.2 2.4 %collective-permute-start = (bf16[4,1,128]{2,1,0:T(2,128)(2,1)S(1)}, bf16[4,1,128]{2,1,0:T(2,128)(2,1)S(1)}, u32[]{:S(2)}, u32[]{:S(2)}) collective-permute-start(bf16[4,1,128]{2,1,0:T(2,128)(2,1)S(1)} %get-tuple-element.46), channel_id=1, source_target_pairs={{0,8},{8,16},{16,24},{1,9},{9,17},{17,25},{2,10},{10,18},{18,26},{... | collective-permute-start | bytes 3080 | tf_op jit(solution)/shard_map/ppermute | solution.py:20
  54.6 2.5 %collective-permute-done = bf16[4,1,128]{2,1,0:T(2,128)(2,1)S(1)} collective-permute-done((bf16[4,1,128]{2,1,0:T(2,128)(2,1)S(1)}, bf16[4,1,128]{2,1,0:T(2,128)(2,1)S(1)}, u32[]{:S(2)}, u32[]{:S(2)}) %collective-permute-start) | collective-permute-done | bytes 1056 | tf_op jit(solution)/shard_map/ppermute | solution.py:20
  57.3 3.0 %collective-permute-start.3 = (bf16[4,130,1]{2,1,0:T(8,128)(2,1)S(1)}, bf16[4,130,1]{2,1,0:T(8,128)(2,1)S(1)}, u32[]{:S(2)}, u32[]{:S(2)}) collective-permute-start(bf16[4,130,1]{2,1,0:T(8,128)(2,1)S(1)} %get-tuple-element.39), channel_id=1, source_target_pairs={{2,0},{4,2},{6,4},{3,1},{5,3},{7,5},{10,8},{12,10},{14,12},{11,9},... | collective-permute-start | bytes 3128 | tf_op jit(solution)/shard_map/ppermute | solution.py:22
  60.3 1.3 collective-permute-start.2
  61.6 1.3 collective-permute-done.3
  62.8 4.4 %collective-permute-done.2 = bf16[4,130,1]{2,1,0:T(8,128)(2,1)S(1)} collective-permute-done((bf16[4,130,1]{2,1,0:T(8,128)(2,1)S(1)}, bf16[4,130,1]{2,1,0:T(8,128)(2,1)S(1)}, u32[]{:S(2)}, u32[]{:S(2)}) %collective-permute-start.2) | collective-permute-done | bytes 1072 | tf_op jit(solution)/shard_map/ppermute | solution.py:20
  68.3 1.9 %collective-permute-start.5 = (bf16[4,2,128]{2,1,0:T(2,128)(2,1)S(1)}, bf16[4,2,128]{2,1,0:T(2,128)(2,1)S(1)}, u32[]{:S(2)}, u32[]{:S(2)}) collective-permute-start(bf16[4,2,128]{2,1,0:T(2,128)(2,1)S(1)} %get-tuple-element.45), channel_id=1, source_target_pairs={{8,0},{16,8},{24,16},{9,1},{17,9},{25,17},{10,2},{18,10},{26,18},{... | collective-permute-start | bytes 6152 | tf_op jit(solution)/shard_map/ppermute | solution.py:22
  70.2 2.4 %collective-permute-start.4 = (bf16[4,2,128]{2,1,0:T(2,128)(2,1)S(1)}, bf16[4,2,128]{2,1,0:T(2,128)(2,1)S(1)}, u32[]{:S(2)}, u32[]{:S(2)}) collective-permute-start(bf16[4,2,128]{2,1,0:T(2,128)(2,1)S(1)} %get-tuple-element.44), channel_id=1, source_target_pairs={{0,8},{8,16},{16,24},{1,9},{9,17},{17,25},{2,10},{10,18},{18,26},{... | collective-permute-start | bytes 6152 | tf_op jit(solution)/shard_map/ppermute | solution.py:20
  72.6 2.5 %collective-permute-done.4 = bf16[4,2,128]{2,1,0:T(2,128)(2,1)S(1)} collective-permute-done((bf16[4,2,128]{2,1,0:T(2,128)(2,1)S(1)}, bf16[4,2,128]{2,1,0:T(2,128)(2,1)S(1)}, u32[]{:S(2)}, u32[]{:S(2)}) %collective-permute-start.4) | collective-permute-done | bytes 2080 | tf_op jit(solution)/shard_map/ppermute | solution.py:20
  75.3 3.8 %collective-permute-start.7 = (bf16[4,132,2]{2,1,0:T(8,128)(2,1)S(1)}, bf16[4,132,2]{2,1,0:T(8,128)(2,1)S(1)}, u32[]{:S(2)}, u32[]{:S(2)}) collective-permute-start(bf16[4,132,2]{2,1,0:T(8,128)(2,1)S(1)} %get-tuple-element.37), channel_id=1, source_target_pairs={{2,0},{4,2},{6,4},{3,1},{5,3},{7,5},{10,8},{12,10},{14,12},{11,9},... | collective-permute-start | bytes 6344 | tf_op jit(solution)/shard_map/ppermute | solution.py:22
  79.0 1.3 collective-permute-start.6
  80.3 1.3 collective-permute-done.7
  81.6 4.4 %collective-permute-done.6 = bf16[4,132,2]{2,1,0:T(8,128)(2,1)S(1)} collective-permute-done((bf16[4,132,2]{2,1,0:T(8,128)(2,1)S(1)}, bf16[4,132,2]{2,1,0:T(8,128)(2,1)S(1)}, u32[]{:S(2)}, u32[]{:S(2)}) %collective-permute-start.6) | collective-permute-done | bytes 2144 | tf_op jit(solution)/shard_map/ppermute | solution.py:20
  87.0 1.9 %collective-permute-start.9 = (bf16[4,4,128]{2,1,0:T(4,128)(2,1)S(1)}, bf16[4,4,128]{2,1,0:T(4,128)(2,1)S(1)}, u32[]{:S(2)}, u32[]{:S(2)}) collective-permute-start(bf16[4,4,128]{2,1,0:T(4,128)(2,1)S(1)} %get-tuple-element.43), channel_id=1, source_target_pairs={{8,0},{16,8},{24,16},{9,1},{17,9},{25,17},{10,2},{18,10},{26,18},{... | collective-permute-start | bytes 12296 | tf_op jit(solution)/shard_map/ppermute | solution.py:22
  89.0 2.4 %collective-permute-start.8 = (bf16[4,4,128]{2,1,0:T(4,128)(2,1)S(1)}, bf16[4,4,128]{2,1,0:T(4,128)(2,1)S(1)}, u32[]{:S(2)}, u32[]{:S(2)}) collective-permute-start(bf16[4,4,128]{2,1,0:T(4,128)(2,1)S(1)} %get-tuple-element.42), channel_id=1, source_target_pairs={{0,8},{8,16},{16,24},{1,9},{9,17},{17,25},{2,10},{10,18},{18,26},{... | collective-permute-start | bytes 12296 | tf_op jit(solution)/shard_map/ppermute | solution.py:20
  91.4 2.5 %collective-permute-done.8 = bf16[4,4,128]{2,1,0:T(4,128)(2,1)S(1)} collective-permute-done((bf16[4,4,128]{2,1,0:T(4,128)(2,1)S(1)}, bf16[4,4,128]{2,1,0:T(4,128)(2,1)S(1)}, u32[]{:S(2)}, u32[]{:S(2)}) %collective-permute-start.8) | collective-permute-done | bytes 4128 | tf_op jit(solution)/shard_map/ppermute | solution.py:20
  94.1 3.9 %collective-permute-start.11 = (bf16[4,136,4]{2,1,0:T(8,128)(2,1)S(1)}, bf16[4,136,4]{2,1,0:T(8,128)(2,1)S(1)}, u32[]{:S(2)}, u32[]{:S(2)}) collective-permute-start(bf16[4,136,4]{2,1,0:T(8,128)(2,1)S(1)} %get-tuple-element.35), channel_id=1, source_target_pairs={{2,0},{4,2},{6,4},{3,1},{5,3},{7,5},{10,8},{12,10},{14,12},{11,9},... | collective-permute-start | bytes 13064 | tf_op jit(solution)/shard_map/ppermute | solution.py:22
  98.0 1.3 collective-permute-start.10
  99.3 1.3 collective-permute-done.11
  100.5 4.4 %collective-permute-done.10 = bf16[4,136,4]{2,1,0:T(8,128)(2,1)S(1)} collective-permute-done((bf16[4,136,4]{2,1,0:T(8,128)(2,1)S(1)}, bf16[4,136,4]{2,1,0:T(8,128)(2,1)S(1)}, u32[]{:S(2)}, u32[]{:S(2)}) %collective-permute-start.10) | collective-permute-done | bytes 4384 | tf_op jit(solution)/shard_map/ppermute | solution.py:20
  106.4 1.9 %collective-permute-start.13 = (bf16[4,8,128]{2,1,0:T(8,128)(2,1)S(1)}, bf16[4,8,128]{2,1,0:T(8,128)(2,1)S(1)}, u32[]{:S(2)}, u32[]{:S(2)}) collective-permute-start(bf16[4,8,128]{2,1,0:T(8,128)(2,1)S(1)} %get-tuple-element.41), channel_id=1, source_target_pairs={{8,0},{16,8},{24,16},{9,1},{17,9},{25,17},{10,2},{18,10},{26,18},{... | collective-permute-start | bytes 24584 | tf_op jit(solution)/shard_map/ppermute | solution.py:22
  108.3 2.4 %collective-permute-start.12 = (bf16[4,8,128]{2,1,0:T(8,128)(2,1)S(1)}, bf16[4,8,128]{2,1,0:T(8,128)(2,1)S(1)}, u32[]{:S(2)}, u32[]{:S(2)}) collective-permute-start(bf16[4,8,128]{2,1,0:T(8,128)(2,1)S(1)} %get-tuple-element.40), channel_id=1, source_target_pairs={{0,8},{8,16},{16,24},{1,9},{9,17},{17,25},{2,10},{10,18},{18,26},{... | collective-permute-start | bytes 24584 | tf_op jit(solution)/shard_map/ppermute | solution.py:20
  110.8 2.5 %collective-permute-done.12 = bf16[4,8,128]{2,1,0:T(8,128)(2,1)S(1)} collective-permute-done((bf16[4,8,128]{2,1,0:T(8,128)(2,1)S(1)}, bf16[4,8,128]{2,1,0:T(8,128)(2,1)S(1)}, u32[]{:S(2)}, u32[]{:S(2)}) %collective-permute-start.12) | collective-permute-done | bytes 8224 | tf_op jit(solution)/shard_map/ppermute | solution.py:20
  113.3 0.8 fusion.101
  114.1 2.6 %collective-permute-start.15 = (bf16[4,144,8]{2,1,0:T(8,128)(2,1)}, bf16[4,144,8]{2,1,0:T(8,128)(2,1)}, u32[]{:S(2)}, u32[]{:S(2)}) collective-permute-start(bf16[4,144,8]{2,1,0:T(8,128)(2,1)} %get-tuple-element.33), channel_id=1, source_target_pairs={{2,0},{4,2},{6,4},{3,1},{5,3},{7,5},{10,8},{12,10},{14,12},{11,9},... | collective-permute-start | bytes 27656 | tf_op jit(solution)/shard_map/ppermute | solution.py:22
  116.7 1.3 collective-permute-start.14
  119.0 5.0 %collective-permute-done.14 = bf16[4,144,8]{2,1,0:T(8,128)(2,1)} collective-permute-done((bf16[4,144,8]{2,1,0:T(8,128)(2,1)}, bf16[4,144,8]{2,1,0:T(8,128)(2,1)}, u32[]{:S(2)}, u32[]{:S(2)}) %collective-permute-start.14) | collective-permute-done | bytes 9248 | tf_op jit(solution)/shard_map/ppermute | solution.py:20
  124.0 1.2 maximum_convert_fusion
  126.2 2.5 %fusion.21 = f32[4,128,128]{2,1,0:T(8,128)S(1)} fusion(f32[4,128,128]{2,1,0:T(8,128)S(1)} %copy-done.5, f32[4,144,144]{2,1,0:T(8,128)S(1)} %get-tuple-element.25, f32[4,144,144]{2,1,0:T(8,128)S(1)} %get-tuple-element.24, f32[4,144,144]{2,1,0:T(8,128)S(1)} %get-tuple-element.17, f32[4]{0:T(128)S(1)} %get-tuple-element.66, f32[4]{0:T(128)S(1)} %get-tuple-element.63, ...), kind=kLoop, calls=%fused_computation.54 | loop fusion | flops 2097152 | bytes 3670144 | tf_op jit(solution)/shard_map/sub | solution.py:193
  128.8 7.2 %all_gather.15 = f32[8,128,128]{2,1,0:T(8,128)S(1)} all-gather(f32[4,128,128]{2,1,0:T(8,128)S(1)} %fusion.21), channel_id=1, replica_groups=mesh['fy'=4,'fx'=4,'blk'=2] {'blk'}, dimensions={0}, use_global_device_ids=true | all-gather | bytes 786432 | tf_op jit(solution)/shard_map/all_gather | solution.py:195
  136.2 1.2 select_add_fusion
  137.5 0.7 fusion.109
  139.6 0.6 broadcast_multiply_fusion.4
  142.3 0.9 slice_reduce_fusion
  143.6 0.7 slice.379
  150.4 0.6 slice.400
  152.3 0.7 slice.401
  154.4 0.6 slice.380
  155.1 0.6 slice.373
  156.0 2.0 %subtract_divide_fusion.2 = (f32[1,8]{1,0:T(1,128)S(1)}, f32[1,8]{1,0:T(1,128)S(1)}) fusion(f32[8,8]{1,0:T(8,128)S(1)} %get-tuple-element.74, f32[]{:T(128)} %bitcast.56, f32[]{:T(128)} %bitcast.54, f32[]{:T(128)} %bitcast.53), kind=kLoop, calls=%fused_computation.218 | loop fusion | flops 32 | bytes 140 | tf_op jit(solution)/shard_map/div | solution.py:127
  158.0 0.6 fusion.81
  158.7 0.6 fusion.80
  160.1 0.7 fusion.78
  161.3 0.6 slice.407
  163.1 0.6 fusion.111
  167.8 0.6 fusion.77
  168.6 1.2 subtract_divide_fusion.1
  169.9 0.7 fusion.75
  171.3 0.6 fusion.73
  172.1 0.6 fusion.72
  172.8 0.6 fusion.71
  173.6 0.7 fusion.70
  174.3 0.9 fusion.14
  175.2 0.7 copy.173
  (159 shorter events, 21.1 us)
Async XLA Ops:
  0.0 22.5 %copy-start = (bf16[1,1,2,4,2,128,128]{6,5,4,3,2,1,0:T(8,128)(2,1)S(1)}, bf16[1,1,2,4,2,128,128]{6,5,4,3,2,1,0:T(8,128)(2,1)}, u32[]{:S(2)}) copy-start(bf16[1,1,2,4,2,128,128]{6,5,4,3,2,1,0:T(8,128)(2,1)} %param.10) | copy-start | bytes 1572868
  0.0 0.7 copy-start.10
  0.0 1.7 copy-start.6
  1.0 0.7 copy-start.7
  21.0 0.7 copy-start.8
  24.1 23.6 %all-to-all-start = ((bf16[4,8,4,256]{3,2,1,0:T(4,128)(2,1)}), bf16[4,8,4,256]{3,2,1,0:T(4,128)(2,1)S(1)}, u32[]{:S(2)}, u32[]{:S(2)}) async-start(bf16[4,8,4,256]{3,2,1,0:T(4,128)(2,1)} %copy.154), calls=%async_computation | async-start | bytes 131072 | tf_op jit(solution)/shard_map/all_to_all | solution.py:170
  50.3 4.3 %collective-permute-start.1 = (bf16[4,1,128]{2,1,0:T(2,128)(2,1)S(1)}, bf16[4,1,128]{2,1,0:T(2,128)(2,1)S(1)}, u32[]{:S(2)}, u32[]{:S(2)}) collective-permute-start(bf16[4,1,128]{2,1,0:T(2,128)(2,1)S(1)} %get-tuple-element.47), channel_id=1, source_target_pairs={{8,0},{16,8},{24,16},{9,1},{17,9},{25,17},{10,2},{18,10},{26,18},{... | collective-permute-start | bytes 3080 | tf_op jit(solution)/shard_map/ppermute | solution.py:22
  52.2 4.9 %collective-permute-start = (bf16[4,1,128]{2,1,0:T(2,128)(2,1)S(1)}, bf16[4,1,128]{2,1,0:T(2,128)(2,1)S(1)}, u32[]{:S(2)}, u32[]{:S(2)}) collective-permute-start(bf16[4,1,128]{2,1,0:T(2,128)(2,1)S(1)} %get-tuple-element.46), channel_id=1, source_target_pairs={{0,8},{8,16},{16,24},{1,9},{9,17},{17,25},{2,10},{10,18},{18,26},{... | collective-permute-start | bytes 3080 | tf_op jit(solution)/shard_map/ppermute | solution.py:20
  57.3 5.6 %collective-permute-start.3 = (bf16[4,130,1]{2,1,0:T(8,128)(2,1)S(1)}, bf16[4,130,1]{2,1,0:T(8,128)(2,1)S(1)}, u32[]{:S(2)}, u32[]{:S(2)}) collective-permute-start(bf16[4,130,1]{2,1,0:T(8,128)(2,1)S(1)} %get-tuple-element.39), channel_id=1, source_target_pairs={{2,0},{4,2},{6,4},{3,1},{5,3},{7,5},{10,8},{12,10},{14,12},{11,9},... | collective-permute-start | bytes 3128 | tf_op jit(solution)/shard_map/ppermute | solution.py:22
  60.3 6.9 %collective-permute-start.2 = (bf16[4,130,1]{2,1,0:T(8,128)(2,1)S(1)}, bf16[4,130,1]{2,1,0:T(8,128)(2,1)S(1)}, u32[]{:S(2)}, u32[]{:S(2)}) collective-permute-start(bf16[4,130,1]{2,1,0:T(8,128)(2,1)S(1)} %get-tuple-element.38), channel_id=1, source_target_pairs={{0,2},{2,4},{4,6},{1,3},{3,5},{5,7},{8,10},{10,12},{12,14},{9,11},... | collective-permute-start | bytes 3128 | tf_op jit(solution)/shard_map/ppermute | solution.py:20
  68.3 4.3 %collective-permute-start.5 = (bf16[4,2,128]{2,1,0:T(2,128)(2,1)S(1)}, bf16[4,2,128]{2,1,0:T(2,128)(2,1)S(1)}, u32[]{:S(2)}, u32[]{:S(2)}) collective-permute-start(bf16[4,2,128]{2,1,0:T(2,128)(2,1)S(1)} %get-tuple-element.45), channel_id=1, source_target_pairs={{8,0},{16,8},{24,16},{9,1},{17,9},{25,17},{10,2},{18,10},{26,18},{... | collective-permute-start | bytes 6152 | tf_op jit(solution)/shard_map/ppermute | solution.py:22
  70.2 4.9 %collective-permute-start.4 = (bf16[4,2,128]{2,1,0:T(2,128)(2,1)S(1)}, bf16[4,2,128]{2,1,0:T(2,128)(2,1)S(1)}, u32[]{:S(2)}, u32[]{:S(2)}) collective-permute-start(bf16[4,2,128]{2,1,0:T(2,128)(2,1)S(1)} %get-tuple-element.44), channel_id=1, source_target_pairs={{0,8},{8,16},{16,24},{1,9},{9,17},{17,25},{2,10},{10,18},{18,26},{... | collective-permute-start | bytes 6152 | tf_op jit(solution)/shard_map/ppermute | solution.py:20
  75.3 6.3 %collective-permute-start.7 = (bf16[4,132,2]{2,1,0:T(8,128)(2,1)S(1)}, bf16[4,132,2]{2,1,0:T(8,128)(2,1)S(1)}, u32[]{:S(2)}, u32[]{:S(2)}) collective-permute-start(bf16[4,132,2]{2,1,0:T(8,128)(2,1)S(1)} %get-tuple-element.37), channel_id=1, source_target_pairs={{2,0},{4,2},{6,4},{3,1},{5,3},{7,5},{10,8},{12,10},{14,12},{11,9},... | collective-permute-start | bytes 6344 | tf_op jit(solution)/shard_map/ppermute | solution.py:22
  79.0 6.9 %collective-permute-start.6 = (bf16[4,132,2]{2,1,0:T(8,128)(2,1)S(1)}, bf16[4,132,2]{2,1,0:T(8,128)(2,1)S(1)}, u32[]{:S(2)}, u32[]{:S(2)}) collective-permute-start(bf16[4,132,2]{2,1,0:T(8,128)(2,1)S(1)} %get-tuple-element.36), channel_id=1, source_target_pairs={{0,2},{2,4},{4,6},{1,3},{3,5},{5,7},{8,10},{10,12},{12,14},{9,11},... | collective-permute-start | bytes 6344 | tf_op jit(solution)/shard_map/ppermute | solution.py:20
  86.7 7.2 %copy-start.1 = (f32[4,132,132]{2,1,0:T(8,128)}, f32[4,132,132]{2,1,0:T(8,128)S(1)}, u32[]{:S(2)}) copy-start(f32[4,132,132]{2,1,0:T(8,128)S(1)} %get-tuple-element.29) | copy-start | bytes 836356
  87.0 4.3 %collective-permute-start.9 = (bf16[4,4,128]{2,1,0:T(4,128)(2,1)S(1)}, bf16[4,4,128]{2,1,0:T(4,128)(2,1)S(1)}, u32[]{:S(2)}, u32[]{:S(2)}) collective-permute-start(bf16[4,4,128]{2,1,0:T(4,128)(2,1)S(1)} %get-tuple-element.43), channel_id=1, source_target_pairs={{8,0},{16,8},{24,16},{9,1},{17,9},{25,17},{10,2},{18,10},{26,18},{... | collective-permute-start | bytes 12296 | tf_op jit(solution)/shard_map/ppermute | solution.py:22
  89.0 4.9 %collective-permute-start.8 = (bf16[4,4,128]{2,1,0:T(4,128)(2,1)S(1)}, bf16[4,4,128]{2,1,0:T(4,128)(2,1)S(1)}, u32[]{:S(2)}, u32[]{:S(2)}) collective-permute-start(bf16[4,4,128]{2,1,0:T(4,128)(2,1)S(1)} %get-tuple-element.42), channel_id=1, source_target_pairs={{0,8},{8,16},{16,24},{1,9},{9,17},{17,25},{2,10},{10,18},{18,26},{... | collective-permute-start | bytes 12296 | tf_op jit(solution)/shard_map/ppermute | solution.py:20
  94.1 6.5 %collective-permute-start.11 = (bf16[4,136,4]{2,1,0:T(8,128)(2,1)S(1)}, bf16[4,136,4]{2,1,0:T(8,128)(2,1)S(1)}, u32[]{:S(2)}, u32[]{:S(2)}) collective-permute-start(bf16[4,136,4]{2,1,0:T(8,128)(2,1)S(1)} %get-tuple-element.35), channel_id=1, source_target_pairs={{2,0},{4,2},{6,4},{3,1},{5,3},{7,5},{10,8},{12,10},{14,12},{11,9},... | collective-permute-start | bytes 13064 | tf_op jit(solution)/shard_map/ppermute | solution.py:22
  98.0 6.9 %collective-permute-start.10 = (bf16[4,136,4]{2,1,0:T(8,128)(2,1)S(1)}, bf16[4,136,4]{2,1,0:T(8,128)(2,1)S(1)}, u32[]{:S(2)}, u32[]{:S(2)}) collective-permute-start(bf16[4,136,4]{2,1,0:T(8,128)(2,1)S(1)} %get-tuple-element.34), channel_id=1, source_target_pairs={{0,2},{2,4},{4,6},{1,3},{3,5},{5,7},{8,10},{10,12},{12,14},{9,11},... | collective-permute-start | bytes 13064 | tf_op jit(solution)/shard_map/ppermute | solution.py:20
  105.3 0.8 copy-start.2
  105.6 7.7 %copy-start.3 = (f32[4,136,136]{2,1,0:T(8,128)}, f32[4,136,136]{2,1,0:T(8,128)S(1)}, u32[]{:S(2)}) copy-start(f32[4,136,136]{2,1,0:T(8,128)S(1)} %get-tuple-element.26) | copy-start | bytes 887812
  105.6 7.7 %copy-start.4 = (f32[4,136,136]{2,1,0:T(8,128)}, f32[4,136,136]{2,1,0:T(8,128)S(1)}, u32[]{:S(2)}) copy-start(f32[4,136,136]{2,1,0:T(8,128)S(1)} %get-tuple-element.27) | copy-start | bytes 887812
  106.4 4.4 %copy-start.9 = (f32[4,4]{1,0:T(4,128)S(1)}, f32[4,4]{1,0:T(4,128)}, u32[]{:S(2)}) copy-start(f32[4,4]{1,0:T(4,128)} %param.14) | copy-start | bytes 196
  106.4 4.4 %collective-permute-start.13 = (bf16[4,8,128]{2,1,0:T(8,128)(2,1)S(1)}, bf16[4,8,128]{2,1,0:T(8,128)(2,1)S(1)}, u32[]{:S(2)}, u32[]{:S(2)}) collective-permute-start(bf16[4,8,128]{2,1,0:T(8,128)(2,1)S(1)} %get-tuple-element.41), channel_id=1, source_target_pairs={{8,0},{16,8},{24,16},{9,1},{17,9},{25,17},{10,2},{18,10},{26,18},{... | collective-permute-start | bytes 24584 | tf_op jit(solution)/shard_map/ppermute | solution.py:22
  108.3 5.0 %collective-permute-start.12 = (bf16[4,8,128]{2,1,0:T(8,128)(2,1)S(1)}, bf16[4,8,128]{2,1,0:T(8,128)(2,1)S(1)}, u32[]{:S(2)}, u32[]{:S(2)}) collective-permute-start(bf16[4,8,128]{2,1,0:T(8,128)(2,1)S(1)} %get-tuple-element.40), channel_id=1, source_target_pairs={{0,8},{8,16},{16,24},{1,9},{9,17},{17,25},{2,10},{10,18},{18,26},{... | collective-permute-start | bytes 24584 | tf_op jit(solution)/shard_map/ppermute | solution.py:20
  114.1 4.9 %collective-permute-start.15 = (bf16[4,144,8]{2,1,0:T(8,128)(2,1)}, bf16[4,144,8]{2,1,0:T(8,128)(2,1)}, u32[]{:S(2)}, u32[]{:S(2)}) collective-permute-start(bf16[4,144,8]{2,1,0:T(8,128)(2,1)} %get-tuple-element.33), channel_id=1, source_target_pairs={{2,0},{4,2},{6,4},{3,1},{5,3},{7,5},{10,8},{12,10},{14,12},{11,9},... | collective-permute-start | bytes 27656 | tf_op jit(solution)/shard_map/ppermute | solution.py:22
  116.7 7.3 %collective-permute-start.14 = (bf16[4,144,8]{2,1,0:T(8,128)(2,1)}, bf16[4,144,8]{2,1,0:T(8,128)(2,1)}, u32[]{:S(2)}, u32[]{:S(2)}) collective-permute-start(bf16[4,144,8]{2,1,0:T(8,128)(2,1)} %get-tuple-element.32), channel_id=1, source_target_pairs={{0,2},{2,4},{4,6},{1,3},{3,5},{5,7},{8,10},{10,12},{12,14},{9,11},... | collective-permute-start | bytes 27656 | tf_op jit(solution)/shard_map/ppermute | solution.py:20
  125.3 1.0 copy-start.5
where the time goes:
time: 177 us; the launch traced here: 176 us
  blocking collectives  41.9 us (24%)
  starting transfers between devices  40.7 us (23%)
  waiting for transfers between devices  32.3 us (18%)
  other arithmetic  21.5 us (12%)
  local copies, waits for them, and re-layouts  20.3 us (11%)
  between operations  13 us (7%)
  matrix products  6.1 us (3%)
    ppermute x8, waiting for transfers between devices, extended(): lax.ppermute(tail, axis, [(i, (i + 1) % count) for i in range(ends)])  28.2 us
    ppermute x8, starting transfers between devices, extended(): lax.ppermute(head, axis, [((i + 1) % count, i) for i in range(ends)])  20.9 us
    all_gather x1, blocking collectives, body(): row_images = lax.all_gather(sky_image[None], 'fx', axis=0, tiled=True)  16.4 us
    ppermute x8, starting transfers between devices, extended(): lax.ppermute(tail, axis, [(i, (i + 1) % count) for i in range(ends)])  14.8 us
    all_gather x1, blocking collectives, body(): lax.all_gather(block_tiles[None], 'fx', axis=0, tiled=True)  10.6 us
    all_gather x1, blocking collectives, body(): lax.all_gather(chosen_ids[None], 'fx', axis=0, tiled=True)  7.6 us
    all_gather x1, blocking collectives, body(): all_channels = lax.all_gather(shrunk, 'blk', axis=0, tiled=True)  7.22 us
    all_to_all x1, starting transfers between devices, body(): lax.all_to_all(outgoing.astype(jnp.bfloat16), 'fx', split_axis=0, concat_...  5.09 us
  transfers between devices with their start and end apart: 17, of which 12 were waited for; matrix products, arithmetic and copies ran while one was open for 0% of the time, Pallas kernels for 0%

commit v1 on v0

v1 whole, which is shorter than its diff:
```python
import functools
import math

import jax
import jax.numpy as jnp
import numpy as np
from jax import lax
from jax.experimental import pallas as pl
from jax.experimental.pallas import tpu as pltpu
from jax.sharding import PartitionSpec as P

MESH = pl.DeviceIdType.MESH
descent_step = 2.0
f32, bf16 = jnp.float32, jnp.bfloat16


def dft_tables(length):
    positions = np.arange(length)
    angles = (positions[:, None] * positions[None, :] % length) * (2.0 * math.pi / length)
    scaling = 1.0 / math.sqrt(length)
    cosine, sinus = np.cos(angles) * scaling, np.sin(angles) * scaling
    left = np.concatenate([cosine, -sinus], axis=0)
    right = np.concatenate(
        [np.concatenate([cosine, -sinus], axis=1), np.concatenate([sinus, cosine], axis=1)], axis=0
    )
    return jnp.asarray(left.astype(np.float32), bf16), jnp.asarray(right.astype(np.float32), bf16)


def dot(a, b):
    return jnp.dot(a, b, preferred_element_type=f32)


def dot_nt(a, b):
    return lax.dot_general(a, b, (((1,), (1,)), ((), ())), preferred_element_type=f32)


def corners():
    return [(dy, dx) for dy in (-1, 0, 1) for dx in (-1, 0, 1) if (dy, dx) != (0, 0)]


def kernel(
    nfy, nfx, nblk, halo,
    rows_s, list_s, count_s, bound_s, weight_s,
    sky_h, vis_h, w_h, left_h, right_h,
    out_ref,
    sky, vis, w, left, right, vis8,
    oh_out, oh_in, pick_f, row_out, row_in, con_out, con_in, con_f,
    step_b, pack_l, pack_r, land_t, land_b, land_l, land_r,
    shr_b, shr_in,
    load_sem, oh_s, oh_r, row_s, row_r, con_s, con_r, halo_s, halo_r, blk_s, blk_r,
):
    fy, fx, bk = lax.axis_index("fy"), lax.axis_index("fx"), lax.axis_index("blk")
    _, _, facets, tiles, slots = rows_s.shape
    chans, size, _ = sky.shape
    rows = tiles * slots
    parts = 2 * chans

    loads = [
        pltpu.make_async_copy(src, dst, load_sem.at[i])
        for i, (src, dst) in enumerate(
            [(sky_h, sky), (left_h, left), (right_h, right), (vis_h, vis), (w_h, w)]
        )
    ]
    for load in loads:
        load.start()

    has = {-1: {0: fy > 0, 1: fx > 0}, 1: {0: fy < nfy - 1, 1: fx < nfx - 1}}

    def near(dy, dx):
        cond = None
        for d, axis in ((dy, 0), (dx, 1)):
            if d:
                cond = has[d][axis] if cond is None else jnp.logical_and(cond, has[d][axis])
        return cond

    barrier = pltpu.get_barrier_semaphore()
    for o in range(1, nfx):
        pl.semaphore_signal(
            barrier, inc=1, device_id=(fy, lax.rem(fx + o, nfx), bk), device_id_type=MESH
        )
    for o in range(1, nblk):
        pl.semaphore_signal(
            barrier, inc=1, device_id=(fy, fx, lax.rem(bk + o, nblk)), device_id_type=MESH
        )
    for dy, dx in corners():
        if dy:

            @pl.when(near(dy, dx))
            def _():
                pl.semaphore_signal(
                    barrier, inc=1, device_id=(fy + dy, fx + dx, bk), device_id_type=MESH
                )

    sub = lax.broadcasted_iota(jnp.int32, (rows, size), 0)
    lane = lax.broadcasted_iota(jnp.int32, (rows, size), 1)
    hots = []
    for f in range(facets):
        wanted = jnp.zeros((rows, size), jnp.int32)
        for a in range(tiles):
            for n in range(slots):
                wanted = jnp.where(sub == a * slots + n, rows_s[0, 0, f, a, n], wanted)
        hots.append(jnp.where(wanted == lane, 1.0, 0.0))

    def match(f, o):
        return (list_s[0, 0, f] == lax.rem(fx + o, nfx)).astype(f32)

    for o in range(nfx):
        hot = hots[0] * match(0, o)
        for f in range(1, facets):
            hot = hot + hots[f] * match(f, o)
        if o:
            oh_out[o - 1] = hot
        else:
            oh_in[0] = hot

    waits = 0
    for v in ((fy > 0), (fy < nfy - 1)):
        waits = waits + v.astype(jnp.int32)
    sides = 1 + (fx > 0).astype(jnp.int32) + (fx < nfx - 1).astype(jnp.int32)
    pl.semaphore_wait(barrier, nfx - 1 + nblk - 1 + waits * sides)

    def peer(src, dst, send, recv, o, way):
        target = lax.rem(fx + o, nfx) if way > 0 else lax.rem(fx + nfx - o, nfx)
        return pltpu.make_async_remote_copy(
            src_ref=src, dst_ref=dst, send_sem=send.at[o - 1], recv_sem=recv.at[o - 1],
            device_id=(fy, target, bk), device_id_type=MESH,
        )

    oh_copies = [
        peer(oh_out.at[o - 1], oh_in.at[o], oh_s, oh_r, o, 1) for o in range(1, nfx)
    ]
    for copy in oh_copies:
        copy.start()

    for load in loads[:3]:
        load.wait()
    specs = []
    for c in range(chans):
        half = dot(left[...], sky[c]).astype(bf16)
        half = jnp.concatenate([half[:size], half[size:]], axis=1)
        specs.append(dot(half, right[...]).astype(bf16))

    for copy in oh_copies:
        copy.wait_recv()
    hot = oh_in[...].reshape(nfx * rows, size).astype(bf16)
    for c in range(chans):
        picked = dot(hot, specs[c])
        for p in range(2):
            pick_f[pl.ds(2 * c + p, nfx * rows, stride=parts), :] = picked[
                :, p * size : (p + 1) * size
            ]
    flat = rows * parts
    row_in[0] = pick_f[0:flat].astype(bf16)
    row_copies = []
    for o in range(1, nfx):
        row_out[o - 1] = pick_f[o * flat : (o + 1) * flat].astype(bf16)
    for o in range(1, nfx):
        copy = peer(row_out.at[o - 1], row_in.at[o], row_s, row_r, o, -1)
        copy.start()
        row_copies.append(copy)

    adj = [
        dot_nt(left[p * size : (p + 1) * size], hot).astype(bf16) for p in range(2)
    ]
    for load in loads[3:]:
        load.wait()
    for c in range(chans):
        vis8[2 * c : 2 * c + 2, :] = vis[c].astype(f32)

    for copy in row_copies:
        copy.wait_recv()
    mine = []
    for f in range(facets):
        total = row_in[0].astype(f32) * match(f, 0)
        for o in range(1, nfx):
            total = total + row_in[o].astype(f32) * match(f, o)
        mine.append(total)
    live = count_s[0, 0]
    contrib = [[None] * rows for f in range(facets)]
    span = w.shape[3]
    for a in range(tiles):
        pred = -vis8[:, a * span : (a + 1) * span]
        for f in range(facets):
            for n in range(slots):
                at = a * slots + n
                row = mine[f][at * parts : (at + 1) * parts].astype(bf16)
                pred = pred + dot_nt(row, w[f, a, n])
        slot_id = lax.broadcasted_iota(jnp.int32, (parts, span), 1) + a * span
        residual = jnp.where(slot_id < live, pred, 0.0).astype(bf16)
        for f in range(facets):
            for n in range(slots):
                contrib[f][a * slots + n] = dot(residual, w[f, a, n])
    for o in range(nfx):
        for at in range(0, rows, 2):
            both = []
            for k in (at, at + 1):
                total = contrib[0][k] * match(0, o)
                for f in range(1, facets):
                    total = total + contrib[f][k] * match(f, o)
                both.append(total)
            value = jnp.concatenate(both, axis=0).astype(bf16)
            if o:
                con_out[o - 1, at * parts : (at + 2) * parts] = value
            else:
                con_in[0, at * parts : (at + 2) * parts] = value
    con_copies = []
    for o in range(1, nfx):
        copy = peer(con_out.at[o - 1], con_in.at[o], con_s, con_r, o, 1)
        copy.start()
        con_copies.append(copy)
    for copy in con_copies:
        copy.wait_recv()

    con_f[...] = con_in[...].reshape(nfx * flat, size).astype(f32)
    halves = []
    for c in range(chans):
        grad = jnp.concatenate(
            [con_f[pl.ds(2 * c + p, nfx * rows, stride=parts), :] for p in range(2)], axis=1
        ).astype(bf16)
        halves.append(dot_nt(grad, right[...]).astype(bf16))
    stepped = []
    for c in range(chans):
        grad = dot(adj[0], halves[c][:, :size]) + dot(adj[1], halves[c][:, size:])
        stepped.append(sky[c].astype(f32) - descent_step * grad)

    lane1 = lax.broadcasted_iota(jnp.int32, (size, size), 1)
    seg_l = seg_r = None
    for c in range(chans):
        step_b[c] = stepped[c].astype(bf16)
        to_l = stepped[c] if c == 0 else pltpu.roll(stepped[c], c * halo, 1)
        to_r = stepped[c] if c == 0 else pltpu.roll(stepped[c], size - c * halo, 1)
        seg_l = to_l if c == 0 else jnp.where(lane1 >= c * halo, to_l, seg_l)
        seg_r = to_r if c == 0 else jnp.where(lane1 < size - c * halo, to_r, seg_r)
    pack_l[...] = seg_l.astype(bf16)
    pack_r[...] = seg_r.astype(bf16)
    sources = {
        -1: {-1: pack_l.at[0:halo], 0: step_b.at[:, 0:halo], 1: pack_r.at[0:halo]},
        0: {-1: pack_l, 1: pack_r},
        1: {
            -1: pack_l.at[size - halo : size],
            0: step_b.at[:, size - halo : size],
            1: pack_r.at[size - halo : size],
        },
    }
    spot = {0: slice(0, size), -1: slice(size, size + halo), 1: slice(size + halo, size + 2 * halo)}

    def halo_copy(i, dy, dx):
        if dx == 0:
            dst = land_b if dy < 0 else land_t
        else:
            dst = (land_r if dx < 0 else land_l).at[spot[dy]]
        return pltpu.make_async_remote_copy(
            src_ref=sources[dy][dx], dst_ref=dst, send_sem=halo_s.at[i], recv_sem=halo_r.at[i],
            device_id=(fy + dy, fx + dx, bk), device_id_type=MESH,
        )

    for i, (dy, dx) in enumerate(corners()):

        @pl.when(near(dy, dx))
        def _():
            halo_copy(i, dy, dx).start()

    for i, (dy, dx) in enumerate(corners()):

        @pl.when(near(-dy, -dx))
        def _():
            halo_copy(i, dy, dx).wait_recv()

    tall = size + 2 * halo
    wide = 2 * size
    row_id = lax.broadcasted_iota(jnp.int32, (tall, wide), 0)
    col_id = lax.broadcasted_iota(jnp.int32, (tall, wide), 1)
    up, down, west, east = (
        halo * v.astype(jnp.int32) for v in (fy > 0, fy < nfy - 1, fx > 0, fx < nfx - 1)
    )
    inside = jnp.logical_and(
        jnp.logical_or(row_id < size + down, row_id >= tall - up),
        jnp.logical_or(col_id < size + east, col_id >= wide - west),
    )
    lane2 = lax.broadcasted_iota(jnp.int32, (tall, size), 1)
    from_l, from_r = land_l[...].astype(f32), land_r[...].astype(f32)
    levels = bound_s.shape[0]
    shrunk = []
    blk_copies = []
    for c in range(chans):
        own = jnp.concatenate(
            [stepped[c], land_b[c].astype(f32), land_t[c].astype(f32)], axis=0
        )
        right_part = from_r if c == 0 else pltpu.roll(from_r, size - c * halo, 1)
        left_part = from_l if c == 0 else pltpu.roll(from_l, c * halo, 1)
        beside = jnp.where(lane2 < size // 2, right_part, left_part)
        coarse = jnp.where(inside, jnp.concatenate([own, beside], axis=1), 0.0)
        clipped = None
        for level in range(levels):
            stride = 2**level
            smooth = (
                pltpu.roll(coarse, stride, 0) + 2.0 * coarse + pltpu.roll(coarse, tall - stride, 0)
            ) * 0.25
            smooth = (
                pltpu.roll(smooth, stride, 1) + 2.0 * smooth + pltpu.roll(smooth, wide - stride, 1)
            ) * 0.25
            bound = bound_s[level, c]
            detail = coarse[:size, :size] - smooth[:size, :size]
            detail = jnp.minimum(jnp.maximum(detail, -bound), bound)
            clipped = detail if level == 0 else clipped + detail
            if level < levels - 1:
                coarse = jnp.where(inside, smooth, 0.0)
        value = stepped[c] - clipped
        shrunk.append(value)
        shr_b[c] = value.astype(bf16)
        for o in range(1, nblk):
            copy = pltpu.make_async_remote_copy(
                src_ref=shr_b.at[c], dst_ref=shr_in.at[o - 1, c],
                send_sem=blk_s.at[o - 1, c], recv_sem=blk_r.at[o - 1, c],
                device_id=(fy, fx, lax.rem(bk + o, nblk)), device_id_type=MESH,
            )
            copy.start()
            blk_copies.append(copy)
    for copy in blk_copies:
        copy.wait_recv()
    everyone = list(shrunk)
    for o in range(1, nblk):
        for c in range(chans):
            everyone.append(shr_in[o - 1, c].astype(f32))

    total = len(everyone)
    part = {}
    for c in range(total):
        for d in range(c, total):
            prod = everyone[c] * everyone[d]
            part[c, d] = jnp.sum(prod, axis=0, keepdims=True)
    gram = []
    for c in range(total):
        line = jnp.concatenate([part[min(c, d), max(c, d)] for d in range(total)], axis=0)
        gram.append(jnp.broadcast_to(jnp.sum(line, axis=1, keepdims=True), (total, size)))
    offset = weight_s[0] * float(size * size)
    subs = lax.broadcasted_iota(jnp.int32, (total, size), 0)
    lhs = [g + jnp.where(subs == c, offset, 0.0) for c, g in enumerate(gram)]
    rhs = list(gram)

    def column(x, k):
        return jnp.broadcast_to(x[k : k + 1, :], (total, size))

    for k in range(total):
        inv = 1.0 / column(lhs[k], k)
        lhs[k] = lhs[k] * inv
        rhs[k] = rhs[k] * inv
        for i in range(total):
            if i != k:
                factor = column(lhs[i], k)
                lhs[i] = lhs[i] - factor * lhs[k]
                rhs[i] = rhs[i] - factor * rhs[k]
    for d in range(chans):
        acc = None
        for c in range(total):
            term = rhs[c][d : d + 1, :] * everyone[c]
            acc = term if acc is None else acc + term
        out_ref[d] = acc

    for copy in oh_copies + row_copies + con_copies + blk_copies:
        copy.wait_send()
    for i, (dy, dx) in enumerate(corners()):

        @pl.when(near(dy, dx))
        def _():
            halo_copy(i, dy, dx).wait_send()


def body(
    nfy, nfx, nblk,
    sky_image, vis_data, interp_weights, tile_rows, facet_list, vis_count,
    wavelet_threshold, spectral_weight,
):
    chans, size, _ = sky_image.shape
    facets, tiles, slots, span = interp_weights.shape[2:6]
    left, right = dft_tables(size)
    rows, parts = tiles * slots, 2 * chans
    flat = rows * parts
    halo = 2 ** wavelet_threshold.shape[0]
    tall = size + 2 * halo
    vmem = pltpu.VMEM
    dma = pltpu.SemaphoreType.DMA
    smem_spec = pl.BlockSpec(memory_space=pltpu.SMEM)
    any_spec = pl.BlockSpec(memory_space=pl.ANY)
    return pl.pallas_call(
        functools.partial(kernel, nfy, nfx, nblk, halo),
        out_shape=jax.ShapeDtypeStruct((chans, size, size), f32),
        in_specs=[smem_spec] * 5 + [any_spec] * 5,
        out_specs=pl.BlockSpec(memory_space=pltpu.VMEM),
        scratch_shapes=[
            vmem(sky_image.shape, bf16),
            vmem(vis_data.shape[2:], bf16),
            vmem(interp_weights.shape[2:], bf16),
            vmem(left.shape, bf16),
            vmem(right.shape, bf16),
            vmem((parts, vis_data.shape[4]), f32),
            vmem((nfx - 1, rows, size), f32),
            vmem((nfx, rows, size), f32),
            vmem((nfx * flat, size), f32),
            vmem((nfx - 1, flat, size), bf16),
            vmem((nfx, flat, size), bf16),
            vmem((nfx - 1, flat, size), bf16),
            vmem((nfx, flat, size), bf16),
            vmem((nfx * flat, size), f32),
            vmem((chans, size, size), bf16),
            vmem((size, size), bf16),
            vmem((size, size), bf16),
            vmem((chans, halo, size), bf16),
            vmem((chans, halo, size), bf16),
            vmem((tall, size), bf16),
            vmem((tall, size), bf16),
            vmem((chans, size, size), bf16),
            vmem((nblk - 1, chans, size, size), bf16),
            dma((5,)),
            dma((nfx - 1,)), dma((nfx - 1,)),
            dma((nfx - 1,)), dma((nfx - 1,)),
            dma((nfx - 1,)), dma((nfx - 1,)),
            dma((8,)), dma((8,)),
            dma((nblk - 1, chans)), dma((nblk - 1, chans)),
        ],
        compiler_params=pltpu.CompilerParams(collective_id=0, has_side_effects=True),
    )(
        tile_rows, facet_list, vis_count, wavelet_threshold, spectral_weight.reshape(1),
        sky_image, vis_data.reshape(vis_data.shape[2:]),
        interp_weights.reshape(interp_weights.shape[2:]), left, right,
    )


def solution(mesh):
    in_specs = (
        P("blk", "fy", "fx"),
        P("fy", "fx", "blk", None, None),
        P("fy", "fx", None, None, None, None, None),
        P("fy", "fx", None, None, None),
        P("fy", "fx", None),
        P("fy", "fx"),
        P(None, "blk"),
        P(),
    )
    out_specs = P("blk", "fy", "fx")
    step = functools.partial(body, mesh.shape["fy"], mesh.shape["fx"], mesh.shape["blk"])
    return jax.shard_map(step, mesh=mesh, in_specs=in_specs, out_specs=out_specs, check_vma=False)
```

time: 177 us -> 33.6 us (0.19)
  the two profiles are of different devices: /device:TPU:28 before, /device:TPU:0 now
where the time goes in v1:
time: 33.6 us; the launch traced here: 33.4 us
  Pallas kernels  29 us (86%)
  local copies, waits for them, and re-layouts  3.03 us (9%)
  between operations  1.31 us (4%)
    pallas_call x1, Pallas kernels, body(): pl.pallas_call(functools.partial(kernel, nfy, nfx, nblk, halo), out_shape...  29 us
    unnamed x4, local copies, waits for them, and re-layouts  3.03 us

profile of v1, /device:TPU:0, one launch (start us, length us, event | category | flops | bytes accessed | tf_op | source)
XLA Modules:
  0.0 33.4 jit_solution(11060839261963318709)
XLA Ops:
  1.3 0.0 copy-start
  1.3 0.7 %copy-done = s32[1,1,2,4,2]{3,4,2,1,0:T(2,128)S(1)} copy-done((s32[1,1,2,4,2]{3,4,2,1,0:T(2,128)S(1)}, s32[1,1,2,4,2]{3,4,2,1,0:T(2,128)}, u32[]{:S(2)}) %copy-start) | copy-done | bytes 88
  2.0 0.7 %copy.11.rows_s = s32[1,1,2,4,2]{4,3,2,1,0:T(4,128)} copy(s32[1,1,2,4,2]{3,4,2,1,0:T(2,128)S(1)} %copy-done) | data formatting | bytes 128 | tf_op args[3]
  2.7 29.0 %shard_map.100 = f32[4,128,128]{2,1,0:T(8,128)} custom-call(s32[1,1,2,4,2]{4,3,2,1,0:T(4,128)} %copy.11.rows_s, s32[1,1,2]{2,1,0:T(1,128)} %list_s.1, s32[1,1]{1,0:T(1,128)S(6)} %copy.13.count_s, f32[4,4]{1,0:T(4,128)} %bound_s.1, f32[1]{0:T(128)} %bitcast.3.weight_s, bf16[4,128,128]{2,1,0:T(8,128)(2,1)} %sky_h.1, bf16[4,2,512]{2,1,0:T(2,128)(2,1)} %bitcast.5, ...), custom_call_target="tpu_custom_call" | custom-call | tf_op jit(solution)/shard_map/pallas_call | solution.py:385
  31.7 1.7 %copy.15 = f32[4,128,128]{2,1,0:T(8,128)} copy(f32[4,128,128]{2,1,0:T(8,128)} %shard_map.100) | data formatting | bytes 524288
Async XLA Ops:
  1.3 0.7 %copy-start = (s32[1,1,2,4,2]{3,4,2,1,0:T(2,128)S(1)}, s32[1,1,2,4,2]{3,4,2,1,0:T(2,128)}, u32[]{:S(2)}) copy-start(s32[1,1,2,4,2]{3,4,2,1,0:T(2,128)} %param.13) | copy-start | bytes 196

commit v2 on v1

--- a/solution.py
+++ b/solution.py
@@ -26,6 +26,31 @@
     return jnp.asarray(left.astype(np.float32), bf16), jnp.asarray(right.astype(np.float32), bf16)
 
 
+def smoothing_tables(size, halo, levels, chans):
+    tall = size + 2 * halo
+    gap = np.abs(np.arange(tall)[:, None] - np.arange(tall)[None, :])
+    order = np.r_[halo:tall, 0:halo]
+    row_all, col_all = [], []
+    for before in (0, 1):
+        for after in (0, 1):
+            mask = np.r_[np.full(halo, before), np.ones(size), np.full(halo, after)]
+            kept, lines = np.diag(mask), []
+            for level in range(levels):
+                smooth = 0.5 * (gap == 0) + 0.25 * (gap == 2**level)
+                kept = mask[:, None] * (smooth @ kept)
+                lines.append(kept[halo : halo + size][:, order])
+            row_all.append(np.concatenate(lines, axis=0))
+            col_all.append(np.concatenate([x[:, :size].T for x in lines], axis=1))
+    beside = np.zeros((levels, size, chans, size))
+    for level, x in enumerate(lines):
+        for c in range(chans):
+            beside[level, c * halo : (c + 1) * halo, c] = x[:, size : size + halo].T
+            end = size - c * halo
+            beside[level, end - halo : end, c] = x[:, size + halo :].T
+    beside = beside.reshape(levels, size, chans * size)
+    return [jnp.asarray(np.asarray(x, np.float32), bf16) for x in (row_all, col_all, beside)]
+
+
 def dot(a, b):
     return jnp.dot(a, b, preferred_element_type=f32)
 
@@ -41,28 +66,38 @@
 def kernel(
     nfy, nfx, nblk, halo,
     rows_s, list_s, count_s, bound_s, weight_s,
-    sky_h, vis_h, w_h, left_h, right_h,
+    sky_h, vis_h, w_h, left_h, right_h, rmat_h, cmat_h, beside_h,
     out_ref,
-    sky, vis, w, left, right, vis8,
+    sky, vis, w, left, right, rmat, cmat, beside, vis8,
     oh_out, oh_in, pick_f, row_out, row_in, con_out, con_in, con_f,
     step_b, pack_l, pack_r, land_t, land_b, land_l, land_r,
     shr_b, shr_in,
     load_sem, oh_s, oh_r, row_s, row_r, con_s, con_r, halo_s, halo_r, blk_s, blk_r,
 ):
     fy, fx, bk = lax.axis_index("fy"), lax.axis_index("fx"), lax.axis_index("blk")
-    _, _, facets, tiles, slots = rows_s.shape
+    _, _, facets, slots, tiles = rows_s.shape
     chans, size, _ = sky.shape
     rows = tiles * slots
     parts = 2 * chans
 
+    def edges(at, count):
+        return 2 * (at > 0).astype(jnp.int32) + (at < count - 1).astype(jnp.int32)
+
     loads = [
         pltpu.make_async_copy(src, dst, load_sem.at[i])
         for i, (src, dst) in enumerate(
-            [(sky_h, sky), (left_h, left), (right_h, right), (vis_h, vis), (w_h, w)]
+            [
+                (sky_h, sky), (left_h, left), (right_h, right), (vis_h, vis), (w_h, w),
+                (rmat_h.at[edges(fy, nfy)], rmat), (cmat_h.at[edges(fx, nfx)], cmat),
+                (beside_h, beside),
+            ]
         )
     ]
     for load in loads:
         load.start()
+
+    for land in (land_t, land_b, land_l, land_r):
+        land[...] = jnp.zeros(land.shape, bf16)
 
     has = {-1: {0: fy > 0, 1: fx > 0}, 1: {0: fy < nfy - 1, 1: fx < nfx - 1}}
 
@@ -98,7 +133,7 @@
         wanted = jnp.zeros((rows, size), jnp.int32)
         for a in range(tiles):
             for n in range(slots):
-                wanted = jnp.where(sub == a * slots + n, rows_s[0, 0, f, a, n], wanted)
+                wanted = jnp.where(sub == a * slots + n, rows_s[0, 0, f, n, a], wanted)
         hots.append(jnp.where(wanted == lane, 1.0, 0.0))
 
     def match(f, o):
@@ -266,45 +301,39 @@
         def _():
             halo_copy(i, dy, dx).wait_recv()
 
-    tall = size + 2 * halo
-    wide = 2 * size
-    row_id = lax.broadcasted_iota(jnp.int32, (tall, wide), 0)
-    col_id = lax.broadcasted_iota(jnp.int32, (tall, wide), 1)
-    up, down, west, east = (
-        halo * v.astype(jnp.int32) for v in (fy > 0, fy < nfy - 1, fx > 0, fx < nfx - 1)
-    )
-    inside = jnp.logical_and(
-        jnp.logical_or(row_id < size + down, row_id >= tall - up),
-        jnp.logical_or(col_id < size + east, col_id >= wide - west),
-    )
-    lane2 = lax.broadcasted_iota(jnp.int32, (tall, size), 1)
-    from_l, from_r = land_l[...].astype(f32), land_r[...].astype(f32)
     levels = bound_s.shape[0]
+    side = lax.broadcasted_iota(jnp.int32, land_l.shape, 1)
+    packed = jnp.where(
+        side < size // 2, land_r[...].astype(f32), land_l[...].astype(f32)
+    ).astype(bf16)
+    across = dot(rmat[...], packed).astype(bf16)
+    from_beside = [
+        dot(across[l * size : (l + 1) * size], beside[l]) for l in range(levels)
+    ]
     shrunk = []
     blk_copies = []
     for c in range(chans):
-        own = jnp.concatenate(
-            [stepped[c], land_b[c].astype(f32), land_t[c].astype(f32)], axis=0
-        )
-        right_part = from_r if c == 0 else pltpu.roll(from_r, size - c * halo, 1)
-        left_part = from_l if c == 0 else pltpu.roll(from_l, c * halo, 1)
-        beside = jnp.where(lane2 < size // 2, right_part, left_part)
-        coarse = jnp.where(inside, jnp.concatenate([own, beside], axis=1), 0.0)
-        clipped = None
-        for level in range(levels):
-            stride = 2**level
-            smooth = (
-                pltpu.roll(coarse, stride, 0) + 2.0 * coarse + pltpu.roll(coarse, tall - stride, 0)
-            ) * 0.25
-            smooth = (
-                pltpu.roll(smooth, stride, 1) + 2.0 * smooth + pltpu.roll(smooth, wide - stride, 1)
-            ) * 0.25
-            bound = bound_s[level, c]
-            detail = coarse[:size, :size] - smooth[:size, :size]
-            detail = jnp.minimum(jnp.maximum(detail, -bound), bound)
-            clipped = detail if level == 0 else clipped + detail
-            if level < levels - 1:
-                coarse = jnp.where(inside, smooth, 0.0)
+        if c % 2 == 0:
+            pair = jnp.concatenate(
+                [
+                    jnp.concatenate([step_b[d], land_b[d], land_t[d]], axis=0)
+                    for d in range(c, min(c + 2, chans))
+                ],
+                axis=1,
+            )
+            down = dot(rmat[...], pair).astype(bf16)
+        at = (c % 2) * size
+        coarse, clipped = stepped[c], None
+        for l in range(levels):
+            smooth = dot(
+                down[l * size : (l + 1) * size, at : at + size],
+                cmat[:, l * size : (l + 1) * size],
+            )
+            smooth = smooth + from_beside[l][:, c * size : (c + 1) * size]
+            bound = bound_s[l, c]
+            detail = jnp.minimum(jnp.maximum(coarse - smooth, -bound), bound)
+            clipped = detail if l == 0 else clipped + detail
+            coarse = smooth
         value = stepped[c] - clipped
         shrunk.append(value)
         shr_b[c] = value.astype(bf16)
@@ -374,9 +403,11 @@
     chans, size, _ = sky_image.shape
     facets, tiles, slots, span = interp_weights.shape[2:6]
     left, right = dft_tables(size)
+    levels = wavelet_threshold.shape[0]
     rows, parts = tiles * slots, 2 * chans
     flat = rows * parts
-    halo = 2 ** wavelet_threshold.shape[0]
+    halo = 2**levels
+    rmat, cmat, beside = smoothing_tables(size, halo, levels, chans)
     tall = size + 2 * halo
     vmem = pltpu.VMEM
     dma = pltpu.SemaphoreType.DMA
@@ -385,7 +416,7 @@
     return pl.pallas_call(
         functools.partial(kernel, nfy, nfx, nblk, halo),
         out_shape=jax.ShapeDtypeStruct((chans, size, size), f32),
-        in_specs=[smem_spec] * 5 + [any_spec] * 5,
+        in_specs=[smem_spec] * 5 + [any_spec] * 8,
         out_specs=pl.BlockSpec(memory_space=pltpu.VMEM),
         scratch_shapes=[
             vmem(sky_image.shape, bf16),
@@ -393,6 +424,9 @@
             vmem(interp_weights.shape[2:], bf16),
             vmem(left.shape, bf16),
             vmem(right.shape, bf16),
+            vmem(rmat.shape[1:], bf16),
+            vmem(cmat.shape[1:], bf16),
+            vmem(beside.shape, bf16),
             vmem((parts, vis_data.shape[4]), f32),
             vmem((nfx - 1, rows, size), f32),
             vmem((nfx, rows, size), f32),
@@ -411,7 +445,7 @@
             vmem((tall, size), bf16),
             vmem((chans, size, size), bf16),
             vmem((nblk - 1, chans, size, size), bf16),
-            dma((5,)),
+            dma((8,)),
             dma((nfx - 1,)), dma((nfx - 1,)),
             dma((nfx - 1,)), dma((nfx - 1,)),
             dma((nfx - 1,)), dma((nfx - 1,)),
@@ -420,9 +454,10 @@
         ],
         compiler_params=pltpu.CompilerParams(collective_id=0, has_side_effects=True),
     )(
-        tile_rows, facet_list, vis_count, wavelet_threshold, spectral_weight.reshape(1),
+        tile_rows.swapaxes(3, 4), facet_list, vis_count, wavelet_threshold, spectral_weight.reshape(1),
         sky_image, vis_data.reshape(vis_data.shape[2:]),
         interp_weights.reshape(interp_weights.shape[2:]), left, right,
+        rmat, cmat, beside,
     )
 
 

time: 33.6 us -> 32.2 us (0.958)
  local copies, waits for them, and re-layouts: 3.03 us -> 1.67 us
    unnamed x4 -> x1, local copies, waits for them, and re-layouts: 3.03 us -> 1.67 us
where the time goes in v2:
time: 32.2 us; the launch traced here: 32 us
  Pallas kernels  29 us (90%)
  local copies, waits for them, and re-layouts  1.67 us (5%)
  between operations  1.3 us (4%)
    pallas_call x1, Pallas kernels, body(): pl.pallas_call(functools.partial(kernel, nfy, nfx, nblk, halo), out_shape...  29 us
    unnamed x1, local copies, waits for them, and re-layouts  1.67 us

profile of v2, /device:TPU:0, one launch (start us, length us, event | category | flops | bytes accessed | tf_op | source)
XLA Modules:
  0.0 32.0 jit_solution(13204351681965881108)
XLA Ops:
  1.3 29.0 %shard_map.127 = f32[4,128,128]{2,1,0:T(8,128)} custom-call(s32[1,1,2,2,4]{4,3,2,1,0:T(2,128)} %bitcast.7, s32[1,1,2]{2,1,0:T(1,128)} %list_s.1, s32[1,1]{1,0:T(1,128)S(6)} %copy.15.count_s, f32[4,4]{1,0:T(4,128)} %bound_s.1, f32[1]{0:T(128)} %bitcast.4.weight_s, bf16[4,128,128]{2,1,0:T(8,128)(2,1)} %sky_h.1, bf16[4,2,512]{2,1,0:T(2,128)(2,1)} %bitcast.6, ...), custom_call_target="tpu_custom_call" | custom-call | tf_op jit(solution)/shard_map/pallas_call | solution.py:416
  30.3 1.7 %copy.17 = f32[4,128,128]{2,1,0:T(8,128)} copy(f32[4,128,128]{2,1,0:T(8,128)} %shard_map.127) | data formatting | bytes 524288

commit v3 on v2

--- a/solution.py
+++ b/solution.py
@@ -48,7 +48,8 @@
             end = size - c * halo
             beside[level, end - halo : end, c] = x[:, size + halo :].T
     beside = beside.reshape(levels, size, chans * size)
-    return [jnp.asarray(np.asarray(x, np.float32), bf16) for x in (row_all, col_all, beside)]
+    rim = np.concatenate([np.r_[x[:halo], x[size - halo :]][:, size:] for x in lines], axis=0)
+    return [jnp.asarray(np.asarray(x, np.float32), bf16) for x in (row_all, col_all, beside, rim)]
 
 
 def dot(a, b):
@@ -66,12 +67,12 @@
 def kernel(
     nfy, nfx, nblk, halo,
     rows_s, list_s, count_s, bound_s, weight_s,
-    sky_h, vis_h, w_h, left_h, right_h, rmat_h, cmat_h, beside_h,
+    sky_h, vis_h, w_h, left_h, right_h, rmat_h, cmat_h, beside_h, rim_h,
     out_ref,
-    sky, vis, w, left, right, rmat, cmat, beside, vis8,
+    sky, vis, w, left, right, rmat, cmat, beside, rim, vis8,
     oh_out, oh_in, pick_f, row_out, row_in, con_out, con_in, con_f,
     step_b, pack_l, pack_r, land_t, land_b, land_l, land_r,
-    shr_b, shr_in,
+    shr_b, shr_in, edge_b, edge_in, side_b, side_in,
     load_sem, oh_s, oh_r, row_s, row_r, con_s, con_r, halo_s, halo_r, blk_s, blk_r,
 ):
     fy, fx, bk = lax.axis_index("fy"), lax.axis_index("fx"), lax.axis_index("blk")
@@ -89,7 +90,7 @@
             [
                 (sky_h, sky), (left_h, left), (right_h, right), (vis_h, vis), (w_h, w),
                 (rmat_h.at[edges(fy, nfy)], rmat), (cmat_h.at[edges(fx, nfx)], cmat),
-                (beside_h, beside),
+                (beside_h, beside), (rim_h, rim),
             ]
         )
     ]
@@ -161,11 +162,23 @@
             device_id=(fy, target, bk), device_id_type=MESH,
         )
 
+    def start_all(copies, way):
+        low = fx < nfx // 2
+
+        @pl.when(low if way > 0 else jnp.logical_not(low))
+        def _():
+            for copy in reversed(copies):
+                copy.start()
+
+        @pl.when(jnp.logical_not(low) if way > 0 else low)
+        def _():
+            for copy in copies:
+                copy.start()
+
     oh_copies = [
         peer(oh_out.at[o - 1], oh_in.at[o], oh_s, oh_r, o, 1) for o in range(1, nfx)
     ]
-    for copy in oh_copies:
-        copy.start()
+    start_all(oh_copies, 1)
 
     for load in loads[:3]:
         load.wait()
@@ -190,9 +203,8 @@
     for o in range(1, nfx):
         row_out[o - 1] = pick_f[o * flat : (o + 1) * flat].astype(bf16)
     for o in range(1, nfx):
-        copy = peer(row_out.at[o - 1], row_in.at[o], row_s, row_r, o, -1)
-        copy.start()
-        row_copies.append(copy)
+        row_copies.append(peer(row_out.at[o - 1], row_in.at[o], row_s, row_r, o, -1))
+    start_all(row_copies, -1)
 
     adj = [
         dot_nt(left[p * size : (p + 1) * size], hot).astype(bf16) for p in range(2)
@@ -240,9 +252,8 @@
                 con_in[0, at * parts : (at + 2) * parts] = value
     con_copies = []
     for o in range(1, nfx):
-        copy = peer(con_out.at[o - 1], con_in.at[o], con_s, con_r, o, 1)
-        copy.start()
-        con_copies.append(copy)
+        con_copies.append(peer(con_out.at[o - 1], con_in.at[o], con_s, con_r, o, 1))
+    start_all(con_copies, 1)
     for copy in con_copies:
         copy.wait_recv()
 
@@ -295,13 +306,51 @@
         def _():
             halo_copy(i, dy, dx).start()
 
+    levels = bound_s.shape[0]
+    inner = []
+    for c in range(chans):
+        if c % 2 == 0:
+            pair = jnp.concatenate([step_b[d] for d in range(c, min(c + 2, chans))], axis=1)
+            down = dot(rmat[:, :size], pair).astype(bf16)
+        at = (c % 2) * size
+        inner.append(
+            [
+                dot(
+                    down[l * size : (l + 1) * size, at : at + size],
+                    cmat[:, l * size : (l + 1) * size],
+                )
+                for l in range(levels)
+            ]
+        )
+
+    def shrink(c, smooths):
+        coarse, clipped = stepped[c], None
+        for l, smooth in enumerate(smooths):
+            bound = bound_s[l, c]
+            detail = jnp.minimum(jnp.maximum(coarse - smooth, -bound), bound)
+            clipped = detail if l == 0 else clipped + detail
+            coarse = smooth
+        return stepped[c] - clipped
+
+    def across_blk(src, dst, i, o):
+        return pltpu.make_async_remote_copy(
+            src_ref=src, dst_ref=dst, send_sem=blk_s.at[o - 1, i], recv_sem=blk_r.at[o - 1, i],
+            device_id=(fy, fx, lax.rem(bk + o, nblk)), device_id_type=MESH,
+        )
+
+    blk_copies = []
+    for c in range(chans):
+        shr_b[c] = shrink(c, inner[c])[halo : size - halo].astype(bf16)
+        for o in range(1, nblk):
+            blk_copies.append(across_blk(shr_b.at[c], shr_in.at[o - 1, c], c, o))
+            blk_copies[-1].start()
+
     for i, (dy, dx) in enumerate(corners()):
 
         @pl.when(near(-dy, -dx))
         def _():
             halo_copy(i, dy, dx).wait_recv()
 
-    levels = bound_s.shape[0]
     side = lax.broadcasted_iota(jnp.int32, land_l.shape, 1)
     packed = jnp.where(
         side < size // 2, land_r[...].astype(f32), land_l[...].astype(f32)
@@ -310,54 +359,65 @@
     from_beside = [
         dot(across[l * size : (l + 1) * size], beside[l]) for l in range(levels)
     ]
+    margin = jnp.concatenate(
+        [jnp.concatenate([land_b[c], land_t[c]], axis=0) for c in range(chans)], axis=1
+    )
+    margin = dot(rim[...], margin).astype(bf16)
+    two = 2 * halo
+    from_rim = [
+        dot(
+            jnp.concatenate(
+                [
+                    margin[l * two : (l + 1) * two, c * size : (c + 1) * size]
+                    for c in range(chans)
+                ],
+                axis=0,
+            ),
+            cmat[:, l * size : (l + 1) * size],
+        )
+        for l in range(levels)
+    ]
     shrunk = []
-    blk_copies = []
-    for c in range(chans):
-        if c % 2 == 0:
-            pair = jnp.concatenate(
-                [
-                    jnp.concatenate([step_b[d], land_b[d], land_t[d]], axis=0)
-                    for d in range(c, min(c + 2, chans))
-                ],
-                axis=1,
-            )
-            down = dot(rmat[...], pair).astype(bf16)
-        at = (c % 2) * size
-        coarse, clipped = stepped[c], None
+    for c in range(chans):
+        smooths = []
         for l in range(levels):
-            smooth = dot(
-                down[l * size : (l + 1) * size, at : at + size],
-                cmat[:, l * size : (l + 1) * size],
-            )
-            smooth = smooth + from_beside[l][:, c * size : (c + 1) * size]
-            bound = bound_s[l, c]
-            detail = jnp.minimum(jnp.maximum(coarse - smooth, -bound), bound)
-            clipped = detail if l == 0 else clipped + detail
-            coarse = smooth
-        value = stepped[c] - clipped
+            smooth = inner[c][l] + from_beside[l][:, c * size : (c + 1) * size]
+            top = smooth[:halo] + from_rim[l][c * two : c * two + halo]
+            bottom = smooth[size - halo :] + from_rim[l][c * two + halo : (c + 1) * two]
+            smooths.append(jnp.concatenate([top, smooth[halo : size - halo], bottom], axis=0))
+        value = shrink(c, smooths)
         shrunk.append(value)
-        shr_b[c] = value.astype(bf16)
-        for o in range(1, nblk):
-            copy = pltpu.make_async_remote_copy(
-                src_ref=shr_b.at[c], dst_ref=shr_in.at[o - 1, c],
-                send_sem=blk_s.at[o - 1, c], recv_sem=blk_r.at[o - 1, c],
-                device_id=(fy, fx, lax.rem(bk + o, nblk)), device_id_type=MESH,
-            )
-            copy.start()
-            blk_copies.append(copy)
+        edge_b[c] = jnp.concatenate([value[:halo], value[size - halo :]], axis=0).astype(bf16)
+        turned = pltpu.roll(value[halo : size - halo], (halo + c * two) % size, 1)
+        sides = turned if c == 0 else jnp.where(lane1[: size - two] >= c * two, turned, sides)
+    side_b[...] = sides.astype(bf16)
+    for o in range(1, nblk):
+        blk_copies.append(across_blk(side_b, side_in.at[o - 1], chans, o))
+        blk_copies[-1].start()
+        blk_copies.append(across_blk(edge_b, edge_in.at[o - 1], chans + 1, o))
+        blk_copies[-1].start()
+    part = {}
+
+    def products(those):
+        for c, d in those:
+            part[c, d] = jnp.sum(everyone[c] * everyone[d], axis=0, keepdims=True)
+
+    everyone = list(shrunk)
+    products([(c, d) for c in range(chans) for d in range(c, chans)])
     for copy in blk_copies:
         copy.wait_recv()
-    everyone = list(shrunk)
+    brink = lax.broadcasted_iota(jnp.int32, (size - two, size), 1)
+    brink = jnp.logical_or(brink < halo, brink >= size - halo)
     for o in range(1, nblk):
+        sides = side_in[o - 1].astype(f32)
         for c in range(chans):
-            everyone.append(shr_in[o - 1, c].astype(f32))
+            edge = edge_in[o - 1, c].astype(f32)
+            turned = pltpu.roll(sides, (2 * size - halo - c * two) % size, 1)
+            middle = jnp.where(brink, turned, shr_in[o - 1, c].astype(f32))
+            everyone.append(jnp.concatenate([edge[:halo], middle, edge[halo:]], axis=0))
 
     total = len(everyone)
-    part = {}
-    for c in range(total):
-        for d in range(c, total):
-            prod = everyone[c] * everyone[d]
-            part[c, d] = jnp.sum(prod, axis=0, keepdims=True)
+    products([(c, d) for c in range(total) for d in range(max(c, chans), total)])
     gram = []
     for c in range(total):
         line = jnp.concatenate([part[min(c, d), max(c, d)] for d in range(total)], axis=0)
@@ -407,7 +467,7 @@
     rows, parts = tiles * slots, 2 * chans
     flat = rows * parts
     halo = 2**levels
-    rmat, cmat, beside = smoothing_tables(size, halo, levels, chans)
+    rmat, cmat, beside, rim = smoothing_tables(size, halo, levels, chans)
     tall = size + 2 * halo
     vmem = pltpu.VMEM
     dma = pltpu.SemaphoreType.DMA
@@ -415,8 +475,8 @@
     any_spec = pl.BlockSpec(memory_space=pl.ANY)
     return pl.pallas_call(
         functools.partial(kernel, nfy, nfx, nblk, halo),
-        out_shape=jax.ShapeDtypeStruct((chans, size, size), f32),
-        in_specs=[smem_spec] * 5 + [any_spec] * 8,
+        out_shape=pltpu.VMEM((chans, size, size), f32),
+        in_specs=[smem_spec] * 5 + [any_spec] * 9,
         out_specs=pl.BlockSpec(memory_space=pltpu.VMEM),
         scratch_shapes=[
             vmem(sky_image.shape, bf16),
@@ -427,6 +487,7 @@
             vmem(rmat.shape[1:], bf16),
             vmem(cmat.shape[1:], bf16),
             vmem(beside.shape, bf16),
+            vmem(rim.shape, bf16),
             vmem((parts, vis_data.shape[4]), f32),
             vmem((nfx - 1, rows, size), f32),
             vmem((nfx, rows, size), f32),
@@ -443,21 +504,25 @@
             vmem((chans, halo, size), bf16),
             vmem((tall, size), bf16),
             vmem((tall, size), bf16),
-            vmem((chans, size, size), bf16),
-            vmem((nblk - 1, chans, size, size), bf16),
-            dma((8,)),
+            vmem((chans, size - 2 * halo, size), bf16),
+            vmem((nblk - 1, chans, size - 2 * halo, size), bf16),
+            vmem((chans, 2 * halo, size), bf16),
+            vmem((nblk - 1, chans, 2 * halo, size), bf16),
+            vmem((size - 2 * halo, size), bf16),
+            vmem((nblk - 1, size - 2 * halo, size), bf16),
+            dma((9,)),
             dma((nfx - 1,)), dma((nfx - 1,)),
             dma((nfx - 1,)), dma((nfx - 1,)),
             dma((nfx - 1,)), dma((nfx - 1,)),
             dma((8,)), dma((8,)),
-            dma((nblk - 1, chans)), dma((nblk - 1, chans)),
+            dma((nblk - 1, chans + 2)), dma((nblk - 1, chans + 2)),
         ],
         compiler_params=pltpu.CompilerParams(collective_id=0, has_side_effects=True),
     )(
         tile_rows.swapaxes(3, 4), facet_list, vis_count, wavelet_threshold, spectral_weight.reshape(1),
         sky_image, vis_data.reshape(vis_data.shape[2:]),
         interp_weights.reshape(interp_weights.shape[2:]), left, right,
-        rmat, cmat, beside,
+        rmat, cmat, beside, rim,
     )
 
 

time: 32.2 us -> 29.1 us (0.904)
  Pallas kernels: 29 us -> 26.9 us
  local copies, waits for them, and re-layouts: 1.67 us -> 0.71 us
    pallas_call x1, Pallas kernels: 29 us -> 26.9 us  [body(): pl.pallas_call(functools.partial(kernel, nfy, nfx, nblk, halo), out_shape...]
    unnamed x1, local copies, waits for them, and re-layouts: 1.67 us -> 0.71 us
where the time goes in v3:
time: 29.1 us; the launch traced here: 28.9 us
  Pallas kernels  26.9 us (92%)
  between operations  1.3 us (4%)
  local copies, waits for them, and re-layouts  0.71 us (2%)
    pallas_call x1, Pallas kernels, body(): pl.pallas_call(functools.partial(kernel, nfy, nfx, nblk, halo), out_shape...  26.9 us
    unnamed x1, local copies, waits for them, and re-layouts  0.71 us

profile of v3, /device:TPU:0, one launch (start us, length us, event | category | flops | bytes accessed | tf_op | source)
XLA Modules:
  0.0 28.9 jit_solution(6539889450483067296)
XLA Ops:
  1.3 26.9 %shard_map.136 = f32[4,128,128]{2,1,0:T(8,128)S(1)} custom-call(s32[1,1,2,2,4]{4,3,2,1,0:T(2,128)} %bitcast.7, s32[1,1,2]{2,1,0:T(1,128)} %list_s.1, s32[1,1]{1,0:T(1,128)S(6)} %copy.17.count_s, f32[4,4]{1,0:T(4,128)} %bound_s.1, f32[1]{0:T(128)} %bitcast.4.weight_s, bf16[4,128,128]{2,1,0:T(8,128)(2,1)} %sky_h.1, bf16[4,2,512]{2,1,0:T(2,128)(2,1)} %bitcast.6, ...), custom_call_target="tpu_custom_call" | custom-call | tf_op jit(solution)/shard_map/pallas_call | solution.py:476
  28.2 0.7 %copy.16 = f32[4,128,128]{2,1,0:T(8,128)} copy(f32[4,128,128]{2,1,0:T(8,128)S(1)} %shard_map.136) | data formatting | bytes 524288

commit v4 on v3

--- a/solution.py
+++ b/solution.py
@@ -66,20 +66,62 @@
 
 def kernel(
     nfy, nfx, nblk, halo,
+    rows_h, list_h, count_h, bound_h, weight_h, sky_h, vis_h, w_h, left_h, right_h, rmat_h, cmat_h, beside_h, rim_h,
+    out_ref,
     rows_s, list_s, count_s, bound_s, weight_s,
-    sky_h, vis_h, w_h, left_h, right_h, rmat_h, cmat_h, beside_h, rim_h,
-    out_ref,
     sky, vis, w, left, right, rmat, cmat, beside, rim, vis8,
     oh_out, oh_in, pick_f, row_out, row_in, con_out, con_in, con_f,
     step_b, pack_l, pack_r, land_t, land_b, land_l, land_r,
     shr_b, shr_in, edge_b, edge_in, side_b, side_in,
-    load_sem, oh_s, oh_r, row_s, row_r, con_s, con_r, halo_s, halo_r, blk_s, blk_r,
+    load_sem, small_sem, oh_s, oh_r, row_s, row_r, con_s, con_r, halo_s, halo_r, blk_s, blk_r,
 ):
     fy, fx, bk = lax.axis_index("fy"), lax.axis_index("fx"), lax.axis_index("blk")
     _, _, facets, slots, tiles = rows_s.shape
     chans, size, _ = sky.shape
     rows = tiles * slots
     parts = 2 * chans
+
+    small = [
+        pltpu.make_async_copy(src, dst, small_sem.at[i])
+        for i, (src, dst) in enumerate(
+            [
+                (rows_h, rows_s), (list_h, list_s), (count_h, count_s), (bound_h, bound_s),
+                (weight_h, weight_s),
+            ]
+        )
+    ]
+    for load in small:
+        load.start()
+
+    for land in (land_t, land_b, land_l, land_r):
+        land[...] = jnp.zeros(land.shape, bf16)
+
+    has = {-1: {0: fy > 0, 1: fx > 0}, 1: {0: fy < nfy - 1, 1: fx < nfx - 1}}
+
+    def near(dy, dx):
+        cond = None
+        for d, axis in ((dy, 0), (dx, 1)):
+            if d:
+                cond = has[d][axis] if cond is None else jnp.logical_and(cond, has[d][axis])
+        return cond
+
+    barrier = pltpu.get_barrier_semaphore()
+    for o in range(1, nfx):
+        pl.semaphore_signal(
+            barrier, inc=1, device_id=(fy, lax.rem(fx + o, nfx), bk), device_id_type=MESH
+        )
+    for o in range(1, nblk):
+        pl.semaphore_signal(
+            barrier, inc=1, device_id=(fy, fx, lax.rem(bk + o, nblk)), device_id_type=MESH
+        )
+    for dy, dx in corners():
+        if dy:
+
+            @pl.when(near(dy, dx))
+            def _():
+                pl.semaphore_signal(
+                    barrier, inc=1, device_id=(fy + dy, fx + dx, bk), device_id_type=MESH
+                )
 
     def edges(at, count):
         return 2 * (at > 0).astype(jnp.int32) + (at < count - 1).astype(jnp.int32)
@@ -97,35 +139,8 @@
     for load in loads:
         load.start()
 
-    for land in (land_t, land_b, land_l, land_r):
-        land[...] = jnp.zeros(land.shape, bf16)
-
-    has = {-1: {0: fy > 0, 1: fx > 0}, 1: {0: fy < nfy - 1, 1: fx < nfx - 1}}
-
-    def near(dy, dx):
-        cond = None
-        for d, axis in ((dy, 0), (dx, 1)):
-            if d:
-                cond = has[d][axis] if cond is None else jnp.logical_and(cond, has[d][axis])
-        return cond
-
-    barrier = pltpu.get_barrier_semaphore()
-    for o in range(1, nfx):
-        pl.semaphore_signal(
-            barrier, inc=1, device_id=(fy, lax.rem(fx + o, nfx), bk), device_id_type=MESH
-        )
-    for o in range(1, nblk):
-        pl.semaphore_signal(
-            barrier, inc=1, device_id=(fy, fx, lax.rem(bk + o, nblk)), device_id_type=MESH
-        )
-    for dy, dx in corners():
-        if dy:
-
-            @pl.when(near(dy, dx))
-            def _():
-                pl.semaphore_signal(
-                    barrier, inc=1, device_id=(fy + dy, fx + dx, bk), device_id_type=MESH
-                )
+    for load in small:
+        load.wait()
 
     sub = lax.broadcasted_iota(jnp.int32, (rows, size), 0)
     lane = lax.broadcasted_iota(jnp.int32, (rows, size), 1)
@@ -471,14 +486,18 @@
     tall = size + 2 * halo
     vmem = pltpu.VMEM
     dma = pltpu.SemaphoreType.DMA
-    smem_spec = pl.BlockSpec(memory_space=pltpu.SMEM)
     any_spec = pl.BlockSpec(memory_space=pl.ANY)
     return pl.pallas_call(
         functools.partial(kernel, nfy, nfx, nblk, halo),
         out_shape=pltpu.VMEM((chans, size, size), f32),
-        in_specs=[smem_spec] * 5 + [any_spec] * 9,
+        in_specs=[any_spec] * 14,
         out_specs=pl.BlockSpec(memory_space=pltpu.VMEM),
         scratch_shapes=[
+            pltpu.SMEM(tile_rows.shape[:3] + (slots, tiles), jnp.int32),
+            pltpu.SMEM(facet_list.shape, jnp.int32),
+            pltpu.SMEM(vis_count.shape, jnp.int32),
+            pltpu.SMEM(wavelet_threshold.shape, f32),
+            pltpu.SMEM((1,), f32),
             vmem(sky_image.shape, bf16),
             vmem(vis_data.shape[2:], bf16),
             vmem(interp_weights.shape[2:], bf16),
@@ -510,7 +529,7 @@
             vmem((nblk - 1, chans, 2 * halo, size), bf16),
             vmem((size - 2 * halo, size), bf16),
             vmem((nblk - 1, size - 2 * halo, size), bf16),
-            dma((9,)),
+            dma((9,)), dma((5,)),
             dma((nfx - 1,)), dma((nfx - 1,)),
             dma((nfx - 1,)), dma((nfx - 1,)),
             dma((nfx - 1,)), dma((nfx - 1,)),

time: 29.1 us -> 28.4 us (0.976)
  Pallas kernels: 26.9 us -> 26.2 us
    pallas_call x1, Pallas kernels: 26.9 us -> 26.2 us  [body(): pl.pallas_call(functools.partial(kernel, nfy, nfx, nblk, halo), out_shape...]
where the time goes in v4:
time: 28.4 us; the launch traced here: 28.2 us
  Pallas kernels  26.2 us (92%)
  between operations  1.3 us (5%)
  local copies, waits for them, and re-layouts  0.71 us (2%)
    pallas_call x1, Pallas kernels, body(): pl.pallas_call(functools.partial(kernel, nfy, nfx, nblk, halo), out_shape...  26.2 us
    unnamed x1, local copies, waits for them, and re-layouts  0.71 us

profile of v4, /device:TPU:0, one launch (start us, length us, event | category | flops | bytes accessed | tf_op | source)
XLA Modules:
  0.0 28.2 jit_solution(16825473123242214063)
XLA Ops:
  1.3 26.2 %shard_map.136 = f32[4,128,128]{2,1,0:T(8,128)S(1)} custom-call(s32[1,1,2,2,4]{4,3,2,1,0:T(2,128)} %bitcast.7, s32[1,1,2]{2,1,0:T(1,128)} %list_h.1, s32[1,1]{1,0:T(1,128)S(6)} %copy.17.count_h, f32[4,4]{1,0:T(4,128)} %bound_h.1, f32[1]{0:T(128)} %bitcast.4.weight_h, bf16[4,128,128]{2,1,0:T(8,128)(2,1)} %sky_h.1, bf16[4,2,512]{2,1,0:T(2,128)(2,1)} %bitcast.6, ...), custom_call_target="tpu_custom_call" | custom-call | tf_op jit(solution)/shard_map/pallas_call | solution.py:490
  27.5 0.7 %copy.16 = f32[4,128,128]{2,1,0:T(8,128)} copy(f32[4,128,128]{2,1,0:T(8,128)S(1)} %shard_map.136) | data formatting | bytes 524288

commit v5 on v4

--- a/solution.py
+++ b/solution.py
@@ -292,18 +292,20 @@
         to_r = stepped[c] if c == 0 else pltpu.roll(stepped[c], size - c * halo, 1)
         seg_l = to_l if c == 0 else jnp.where(lane1 >= c * halo, to_l, seg_l)
         seg_r = to_r if c == 0 else jnp.where(lane1 < size - c * halo, to_r, seg_r)
-    pack_l[...] = seg_l.astype(bf16)
-    pack_r[...] = seg_r.astype(bf16)
+    mid = size // 2
+    first = lane1[:mid] < mid
+    pack_l[...] = jnp.where(first, seg_l[:mid], pltpu.roll(seg_l[mid:], mid, 1)).astype(bf16)
+    pack_r[...] = jnp.where(first, pltpu.roll(seg_r[mid:], mid, 1), seg_r[:mid]).astype(bf16)
     sources = {
         -1: {-1: pack_l.at[0:halo], 0: step_b.at[:, 0:halo], 1: pack_r.at[0:halo]},
         0: {-1: pack_l, 1: pack_r},
         1: {
-            -1: pack_l.at[size - halo : size],
+            -1: pack_l.at[mid - halo : mid],
             0: step_b.at[:, size - halo : size],
-            1: pack_r.at[size - halo : size],
+            1: pack_r.at[mid - halo : mid],
         },
     }
-    spot = {0: slice(0, size), -1: slice(size, size + halo), 1: slice(size + halo, size + 2 * halo)}
+    spot = {0: slice(0, mid), -1: slice(mid, mid + halo), 1: slice(mid + halo, mid + 2 * halo)}
 
     def halo_copy(i, dy, dx):
         if dx == 0:
@@ -366,9 +368,12 @@
         def _():
             halo_copy(i, dy, dx).wait_recv()
 
-    side = lax.broadcasted_iota(jnp.int32, land_l.shape, 1)
-    packed = jnp.where(
-        side < size // 2, land_r[...].astype(f32), land_l[...].astype(f32)
+    side = lax.broadcasted_iota(jnp.int32, land_l.shape, 1) < mid
+    at_r, at_l = land_r[...].astype(f32), land_l[...].astype(f32)
+    upper = jnp.where(side, at_r, at_l)
+    lower = pltpu.roll(jnp.where(side, at_l, at_r), mid, 1)
+    packed = jnp.concatenate(
+        [upper[:mid], lower[:mid], upper[mid : mid + halo], lower[mid + halo :]], axis=0
     ).astype(bf16)
     across = dot(rmat[...], packed).astype(bf16)
     from_beside = [
@@ -517,12 +522,12 @@
             vmem((nfx, flat, size), bf16),
             vmem((nfx * flat, size), f32),
             vmem((chans, size, size), bf16),
-            vmem((size, size), bf16),
-            vmem((size, size), bf16),
+            vmem((size // 2, size), bf16),
+            vmem((size // 2, size), bf16),
             vmem((chans, halo, size), bf16),
             vmem((chans, halo, size), bf16),
-            vmem((tall, size), bf16),
-            vmem((tall, size), bf16),
+            vmem((tall - size // 2, size), bf16),
+            vmem((tall - size // 2, size), bf16),
             vmem((chans, size - 2 * halo, size), bf16),
             vmem((nblk - 1, chans, size - 2 * halo, size), bf16),
             vmem((chans, 2 * halo, size), bf16),

time: 28.4 us -> 28.4 us (level)
  no operation moved by 1% of the time
where the time goes in v5:
time: 28.4 us; the launch traced here: 28.2 us
  Pallas kernels  26.2 us (92%)
  between operations  1.3 us (5%)
  local copies, waits for them, and re-layouts  0.71 us (2%)
    pallas_call x1, Pallas kernels, body(): pl.pallas_call(functools.partial(kernel, nfy, nfx, nblk, halo), out_shape...  26.2 us
    unnamed x1, local copies, waits for them, and re-layouts  0.71 us

profile of v5, /device:TPU:0, one launch (start us, length us, event | category | flops | bytes accessed | tf_op | source)
XLA Modules:
  0.0 28.2 jit_solution(15274579595737659661)
XLA Ops:
  1.3 26.2 %shard_map.136 = f32[4,128,128]{2,1,0:T(8,128)S(1)} custom-call(s32[1,1,2,2,4]{4,3,2,1,0:T(2,128)} %bitcast.7, s32[1,1,2]{2,1,0:T(1,128)} %list_h.1, s32[1,1]{1,0:T(1,128)S(6)} %copy.17.count_h, f32[4,4]{1,0:T(4,128)} %bound_h.1, f32[1]{0:T(128)} %bitcast.4.weight_h, bf16[4,128,128]{2,1,0:T(8,128)(2,1)} %sky_h.1, bf16[4,2,512]{2,1,0:T(2,128)(2,1)} %bitcast.6, ...), custom_call_target="tpu_custom_call" | custom-call | tf_op jit(solution)/shard_map/pallas_call | solution.py:495
  27.5 0.7 %copy.16 = f32[4,128,128]{2,1,0:T(8,128)} copy(f32[4,128,128]{2,1,0:T(8,128)S(1)} %shard_map.136) | data formatting | bytes 524288
